TPU v7x, 256 devices: a whole 4x4x8 slice. The times are simulated.
256 devices in a mesh: row: 64 (over x, z, core), col: 4 (over y).
Axes of the slice: x: 4, y: 4, z: 8, core: 2. Of those that a mesh axis runs over, the one named last changes fastest.
Arguments:
- eigvecs: float32 [16384, 512], P('row', 'col'), may hold values from -6 to 6
- reflectors: float32 [8, 256, 128, 64], P(None, ('row', 'col')), may hold values from -2 to 2, as said below
- factors: float32 [8, 256, 64, 64], P(None, ('row', 'col')), may hold values from -3 to 3, as said below
- order: int32 [8], replicated, may hold values from 0 to 7, each once
- offsets: int32 [8], replicated, may hold values from 0 to 63
Outputs:
- rotated: float32 [16384, 512], P('row', 'col')
Inputs may be any that keep to these rules, and one draw needn't show every extreme that they name: `order`: a permutation of 0 .. 7. Every block map is orthogonal: with V the block of reflectors and T the block of factors, T is upper triangular and T^-1 + T^-T = V^T V. `factors`: upper triangular, paired with reflectors as promised there.
All inputs are finite; a program needn't handle non-finite values.
Results may differ from a plain program's by a relative error of at most 0.0003.
Values sent between devices are 32-bit elements; how exact they have to be, the bound alone decides.
A program may use at most 64 MiB of HBM per device.

v0:
```python
import jax
import jax.numpy as jnp
from jax import lax
from jax.sharding import Mesh
from jax.sharding import PartitionSpec as P

ROW = ("row_0", "row_1", "row_2")
ROW_COL = ("row_0", "row_1", "row_2", "col")


highest = lax.Precision.HIGHEST


def passed_along(block, axis, distance):
    devices = range(lax.axis_size(axis))
    route = [(i - distance, i) for i in devices if i - distance in devices]
    return lax.ppermute(block, axis, route)


def nothing_yet(array, identity):
    return jax.tree.map(
        lambda part, zero: jnp.zeros_like(part) + jnp.asarray(zero, part.dtype), array, identity
    )


def carried_in(array, axes, combine, identity):
    before = start = nothing_yet(array, identity)
    subtotal = array
    for axis in reversed(axes):
        size, position = (lax.axis_size(axis), lax.axis_index(axis))
        pieces = jax.tree.map(lambda part: lax.all_gather(part, axis), subtotal)
        inside, subtotal = (start, start)
        for k in range(size):
            passed = k < position
            subtotal = combine(subtotal, jax.tree.map(lambda part: part[k], pieces))
            inside = jax.tree.map(lambda new, old: jnp.where(passed, new, old), subtotal, inside)
        before = combine(inside, before)
    return before


def reflect(segment, householder, triangle):
    inner = jnp.dot(householder.T, segment, precision=highest, preferred_element_type=jnp.float32)
    inner = jnp.dot(triangle, inner, precision=highest, preferred_element_type=jnp.float32)
    return segment - jnp.dot(
        householder, inner, precision=highest, preferred_element_type=jnp.float32
    )


def sweep_apply(extended, house_set, tri_set, offset):
    block_width = house_set.shape[-1]

    def advance(number, current):
        start = offset + number * block_width
        segment = lax.dynamic_slice_in_dim(current, start, 2 * block_width, 0)
        householder = lax.dynamic_index_in_dim(house_set, number, 0, keepdims=False)
        triangle = lax.dynamic_index_in_dim(tri_set, number, 0, keepdims=False)
        return lax.dynamic_update_slice_in_dim(
            current, reflect(segment, householder, triangle), start, 0
        )

    return lax.fori_loop(0, house_set.shape[0], advance, extended)


def compose(earlier, later):
    first_map = jnp.dot(later[0], earlier[0], precision=highest, preferred_element_type=jnp.float32)
    shifted = (
        jnp.dot(later[0], earlier[1], precision=highest, preferred_element_type=jnp.float32)
        + later[1]
    )
    return (first_map, shifted)


def local(eigvecs, reflectors, factors, order, offsets):
    height = eigvecs.shape[0]
    columns = eigvecs.shape[1]
    block_width = reflectors.shape[-1]
    span_rows = 2 * block_width
    leading = lax.axis_index(ROW) == 0
    identity = jnp.eye(span_rows, dtype=jnp.float32)
    probe = jnp.concatenate([identity, jnp.zeros((height, span_rows), jnp.float32)], 0)
    every_house, every_tri = (
        lax.all_gather(reflectors, "col", axis=1, tiled=True),
        lax.all_gather(factors, "col", axis=1, tiled=True),
    )
    vectors = eigvecs
    for position in range(order.shape[0]):
        stored = order[position]
        offset = offsets[stored]
        house_set = lax.dynamic_index_in_dim(every_house, stored, 0, keepdims=False)
        tri_set = lax.dynamic_index_in_dim(every_tri, stored, 0, keepdims=False)
        next_rows = passed_along(vectors[:span_rows], ROW, -1)
        top_rows = jnp.where(leading, vectors[:span_rows], 0.0)
        extended = jnp.concatenate([top_rows, vectors[span_rows:], next_rows], 0)
        joined = sweep_apply(jnp.concatenate([extended, probe], 1), house_set, tri_set, offset)
        partial_value = joined[:, :columns]
        response = joined[:, columns:]
        transfer = jnp.where(leading, 0.0, response[height:])
        empty = jnp.zeros((span_rows, columns), jnp.float32)
        composed = carried_in((transfer, partial_value[height:]), ROW, compose, (identity, empty))
        incoming = composed[1]
        vectors = partial_value[:height] + jnp.dot(
            response[:height], incoming, precision=highest, preferred_element_type=jnp.float32
        )
    return vectors


def solution(mesh):
    torus = Mesh(
        mesh.devices.reshape(4, 8, 2, mesh.shape["col"]), ("row_0", "row_1", "row_2", "col")
    )
    placed = (P(ROW, "col"), P(None, ROW_COL, None, None), P(None, ROW_COL, None, None), P(), P())
    return jax.shard_map(
        local, mesh=torus, in_specs=placed, out_specs=P(ROW, "col"), check_vma=False
    )
```

profile of v0, /device:TPU:32, one launch (start us, length us, event | category | flops | bytes accessed | tf_op | source)
XLA Modules:
  0.0 849.8 jit_solution(460673301519701262)
XLA Ops:
  7.5 1.9 collective-permute-start
  25.9 20.4 %all_gather.295 = f32[8,4,64,64]{3,2,1,0:T(8,128)S(1)} all-gather(f32[8,1,64,64]{3,2,1,0:T(8,128)S(1)} %copy-done), channel_id=1, replica_groups=mesh['row_0'=4,'row_1'=8,'row_2'=2,'col'=4] {'col'}, dimensions={1}, use_global_device_ids=true | all-gather | bytes 655360 | tf_op jit(solution)/shard_map/all_gather | solution.py:83
  48.0 9.6 %while.104 = (s32[]{:T(128)}, f32[384,256]{1,0:T(8,128)S(1)}, s32[]{:T(128)}, f32[4,128,64]{2,1,0:T(8,128)S(1)}, f32[4,64,64]{2,1,0:T(8,128)S(1)}, /*index=5*/s32[]{:T(128)}, s32[]{:T(128)}, s32[]{:T(128)}, s32[]{:T(128)}) while((s32[]{:T(128)}, f32[384,256]{1,0:T(8,128)S(1)}, s32[]{:T(128)}, f32[4,128,64]{2,1,0:T(8,128)S(1)}, ...), condition=%wide.region_1.2_spmd, body=%wide.region_0.1_spmd.sunk | while | flops 62947336 | bytes 1081519 | solution.py:61
  57.6 1.9 all-gather
  62.0 26.1 %all-gather.4 = f32[1024,128]{1,0:T(8,128)S(1)} all-gather(f32[128,128]{1,0:T(8,128)S(1)} %convolution_add_fusion.124), channel_id=6, replica_groups=mesh['row_0'=4,'row_1'=8,'row_2'=2,'col'=4] {'row_1'}, dimensions={0}, use_global_device_ids=true | all-gather | bytes 589824 | tf_op jit(solution)/shard_map/all_gather | solution.py:31
  88.4 25.5 %all-gather.1 = f32[1024,128]{1,0:T(8,128)S(1)} all-gather(f32[128,128]{1,0:T(8,128)S(1)} %fusion.582), channel_id=3, replica_groups=mesh['row_0'=4,'row_1'=8,'row_2'=2,'col'=4] {'row_1'}, dimensions={0}, use_global_device_ids=true | all-gather | bytes 589824 | tf_op jit(solution)/shard_map/all_gather | solution.py:31
  115.7 12.6 %all-gather.5 = f32[512,128]{1,0:T(8,128)S(1)} all-gather(f32[128,128]{1,0:T(8,128)S(1)} %convolution_add_fusion.117), channel_id=7, replica_groups=mesh['row_0'=4,'row_1'=8,'row_2'=2,'col'=4] {'row_0'}, dimensions={0}, use_global_device_ids=true | all-gather | bytes 327680 | tf_op jit(solution)/shard_map/all_gather | solution.py:31
  129.8 12.3 %all-gather.2 = f32[512,128]{1,0:T(8,128)S(1)} all-gather(f32[128,128]{1,0:T(8,128)S(1)} %fusion.577), channel_id=4, replica_groups=mesh['row_0'=4,'row_1'=8,'row_2'=2,'col'=4] {'row_0'}, dimensions={0}, use_global_device_ids=true | all-gather | bytes 327680 | tf_op jit(solution)/shard_map/all_gather | solution.py:31
  144.3 1.9 collective-permute-start.1
  148.1 9.6 %while.105 = (s32[]{:T(128)}, f32[384,256]{1,0:T(8,128)S(1)}, s32[]{:T(128)}, f32[4,128,64]{2,1,0:T(8,128)S(1)}, f32[4,64,64]{2,1,0:T(8,128)S(1)}, /*index=5*/s32[]{:T(128)}, s32[]{:T(128)}, s32[]{:T(128)}, s32[]{:T(128)}) while((s32[]{:T(128)}, f32[384,256]{1,0:T(8,128)S(1)}, s32[]{:T(128)}, f32[4,128,64]{2,1,0:T(8,128)S(1)}, ...), condition=%wide.region_3.4_spmd, body=%wide.region_2.3_spmd.sunk | while | flops 62947336 | bytes 1081519 | solution.py:61
  157.7 3.6 all-gather.6
  161.7 25.9 %all-gather.7 = f32[1024,128]{1,0:T(8,128)S(1)} all-gather(f32[128,128]{1,0:T(8,128)S(1)} %fusion.554), channel_id=9, replica_groups=mesh['row_0'=4,'row_1'=8,'row_2'=2,'col'=4] {'row_1'}, dimensions={0}, use_global_device_ids=true | all-gather | bytes 589824 | tf_op jit(solution)/shard_map/all_gather | solution.py:31
  187.8 1.9 all-gather.9
  190.1 25.3 %all-gather.10 = f32[1024,128]{1,0:T(8,128)S(1)} all-gather(f32[128,128]{1,0:T(8,128)S(1)} %convolution_add_fusion.109), channel_id=12, replica_groups=mesh['row_0'=4,'row_1'=8,'row_2'=2,'col'=4] {'row_1'}, dimensions={0}, use_global_device_ids=true | all-gather | bytes 589824 | tf_op jit(solution)/shard_map/all_gather | solution.py:31
  217.3 12.3 %all-gather.11 = f32[512,128]{1,0:T(8,128)S(1)} all-gather(f32[128,128]{1,0:T(8,128)S(1)} %convolution_add_fusion.102), channel_id=13, replica_groups=mesh['row_0'=4,'row_1'=8,'row_2'=2,'col'=4] {'row_0'}, dimensions={0}, use_global_device_ids=true | all-gather | bytes 327680 | tf_op jit(solution)/shard_map/all_gather | solution.py:31
  231.3 12.3 %all-gather.8 = f32[512,128]{1,0:T(8,128)S(1)} all-gather(f32[128,128]{1,0:T(8,128)S(1)} %fusion.549), channel_id=10, replica_groups=mesh['row_0'=4,'row_1'=8,'row_2'=2,'col'=4] {'row_0'}, dimensions={0}, use_global_device_ids=true | all-gather | bytes 327680 | tf_op jit(solution)/shard_map/all_gather | solution.py:31
  245.3 1.9 collective-permute-start.2
  249.1 9.0 %while.106 = (s32[]{:T(128)}, f32[384,256]{1,0:T(8,128)S(1)}, s32[]{:T(128)}, f32[4,128,64]{2,1,0:T(8,128)S(1)}, f32[4,64,64]{2,1,0:T(8,128)S(1)}, /*index=5*/s32[]{:T(128)}, s32[]{:T(128)}, s32[]{:T(128)}, s32[]{:T(128)}) while((s32[]{:T(128)}, f32[384,256]{1,0:T(8,128)S(1)}, s32[]{:T(128)}, f32[4,128,64]{2,1,0:T(8,128)S(1)}, ...), condition=%wide.region_5.6_spmd, body=%wide.region_4.5_spmd.sunk | while | flops 62947336 | bytes 1081519 | solution.py:61
  258.2 1.9 all-gather.12
  260.5 26.1 %all-gather.13 = f32[1024,128]{1,0:T(8,128)S(1)} all-gather(f32[128,128]{1,0:T(8,128)S(1)} %fusion.526), channel_id=15, replica_groups=mesh['row_0'=4,'row_1'=8,'row_2'=2,'col'=4] {'row_1'}, dimensions={0}, use_global_device_ids=true | all-gather | bytes 589824 | tf_op jit(solution)/shard_map/all_gather | solution.py:31
  286.7 1.9 all-gather.15
  289.0 25.5 %all-gather.16 = f32[1024,128]{1,0:T(8,128)S(1)} all-gather(f32[128,128]{1,0:T(8,128)S(1)} %convolution_add_fusion.94), channel_id=18, replica_groups=mesh['row_0'=4,'row_1'=8,'row_2'=2,'col'=4] {'row_1'}, dimensions={0}, use_global_device_ids=true | all-gather | bytes 589824 | tf_op jit(solution)/shard_map/all_gather | solution.py:31
  316.4 12.5 %all-gather.17 = f32[512,128]{1,0:T(8,128)S(1)} all-gather(f32[128,128]{1,0:T(8,128)S(1)} %convolution_add_fusion.87), channel_id=19, replica_groups=mesh['row_0'=4,'row_1'=8,'row_2'=2,'col'=4] {'row_0'}, dimensions={0}, use_global_device_ids=true | all-gather | bytes 327680 | tf_op jit(solution)/shard_map/all_gather | solution.py:31
  330.6 12.3 %all-gather.14 = f32[512,128]{1,0:T(8,128)S(1)} all-gather(f32[128,128]{1,0:T(8,128)S(1)} %fusion.521), channel_id=16, replica_groups=mesh['row_0'=4,'row_1'=8,'row_2'=2,'col'=4] {'row_0'}, dimensions={0}, use_global_device_ids=true | all-gather | bytes 327680 | tf_op jit(solution)/shard_map/all_gather | solution.py:31
  344.6 1.9 collective-permute-start.3
  348.5 8.8 %while.107 = (s32[]{:T(128)}, f32[384,256]{1,0:T(8,128)S(1)}, s32[]{:T(128)}, f32[4,128,64]{2,1,0:T(8,128)S(1)}, f32[4,64,64]{2,1,0:T(8,128)S(1)}, /*index=5*/s32[]{:T(128)}, s32[]{:T(128)}, s32[]{:T(128)}, s32[]{:T(128)}) while((s32[]{:T(128)}, f32[384,256]{1,0:T(8,128)S(1)}, s32[]{:T(128)}, f32[4,128,64]{2,1,0:T(8,128)S(1)}, ...), condition=%wide.region_7.8_spmd, body=%wide.region_6.7_spmd.sunk | while | flops 62947336 | bytes 1081519 | solution.py:61
  357.3 2.1 all-gather.18
  359.8 26.6 %all-gather.19 = f32[1024,128]{1,0:T(8,128)S(1)} all-gather(f32[128,128]{1,0:T(8,128)S(1)} %fusion.498), channel_id=21, replica_groups=mesh['row_0'=4,'row_1'=8,'row_2'=2,'col'=4] {'row_1'}, dimensions={0}, use_global_device_ids=true | all-gather | bytes 589824 | tf_op jit(solution)/shard_map/all_gather | solution.py:31
  386.6 1.9 all-gather.21
  388.9 25.3 %all-gather.22 = f32[1024,128]{1,0:T(8,128)S(1)} all-gather(f32[128,128]{1,0:T(8,128)S(1)} %convolution_add_fusion.79), channel_id=24, replica_groups=mesh['row_0'=4,'row_1'=8,'row_2'=2,'col'=4] {'row_1'}, dimensions={0}, use_global_device_ids=true | all-gather | bytes 589824 | tf_op jit(solution)/shard_map/all_gather | solution.py:31
  416.1 12.3 %all-gather.23 = f32[512,128]{1,0:T(8,128)S(1)} all-gather(f32[128,128]{1,0:T(8,128)S(1)} %convolution_add_fusion.72), channel_id=25, replica_groups=mesh['row_0'=4,'row_1'=8,'row_2'=2,'col'=4] {'row_0'}, dimensions={0}, use_global_device_ids=true | all-gather | bytes 327680 | tf_op jit(solution)/shard_map/all_gather | solution.py:31
  430.1 12.3 %all-gather.20 = f32[512,128]{1,0:T(8,128)S(1)} all-gather(f32[128,128]{1,0:T(8,128)S(1)} %fusion.493), channel_id=22, replica_groups=mesh['row_0'=4,'row_1'=8,'row_2'=2,'col'=4] {'row_0'}, dimensions={0}, use_global_device_ids=true | all-gather | bytes 327680 | tf_op jit(solution)/shard_map/all_gather | solution.py:31
  444.2 1.9 collective-permute-start.4
  448.0 9.3 %while.108 = (s32[]{:T(128)}, f32[384,256]{1,0:T(8,128)S(1)}, s32[]{:T(128)}, f32[4,128,64]{2,1,0:T(8,128)S(1)}, f32[4,64,64]{2,1,0:T(8,128)S(1)}, /*index=5*/s32[]{:T(128)}, s32[]{:T(128)}, s32[]{:T(128)}, s32[]{:T(128)}) while((s32[]{:T(128)}, f32[384,256]{1,0:T(8,128)S(1)}, s32[]{:T(128)}, f32[4,128,64]{2,1,0:T(8,128)S(1)}, ...), condition=%wide.region_9.10_spmd, body=%wide.region_8.9_spmd.sunk | while | flops 62947336 | bytes 1081519 | solution.py:61
  457.3 1.9 all-gather.24
  459.6 26.0 %all-gather.25 = f32[1024,128]{1,0:T(8,128)S(1)} all-gather(f32[128,128]{1,0:T(8,128)S(1)} %fusion.470), channel_id=27, replica_groups=mesh['row_0'=4,'row_1'=8,'row_2'=2,'col'=4] {'row_1'}, dimensions={0}, use_global_device_ids=true | all-gather | bytes 589824 | tf_op jit(solution)/shard_map/all_gather | solution.py:31
  485.8 1.9 all-gather.27
  488.1 25.3 %all-gather.28 = f32[1024,128]{1,0:T(8,128)S(1)} all-gather(f32[128,128]{1,0:T(8,128)S(1)} %convolution_add_fusion.64), channel_id=30, replica_groups=mesh['row_0'=4,'row_1'=8,'row_2'=2,'col'=4] {'row_1'}, dimensions={0}, use_global_device_ids=true | all-gather | bytes 589824 | tf_op jit(solution)/shard_map/all_gather | solution.py:31
  515.4 12.3 %all-gather.29 = f32[512,128]{1,0:T(8,128)S(1)} all-gather(f32[128,128]{1,0:T(8,128)S(1)} %convolution_add_fusion.57), channel_id=31, replica_groups=mesh['row_0'=4,'row_1'=8,'row_2'=2,'col'=4] {'row_0'}, dimensions={0}, use_global_device_ids=true | all-gather | bytes 327680 | tf_op jit(solution)/shard_map/all_gather | solution.py:31
  529.4 12.5 %all-gather.26 = f32[512,128]{1,0:T(8,128)S(1)} all-gather(f32[128,128]{1,0:T(8,128)S(1)} %fusion.465), channel_id=28, replica_groups=mesh['row_0'=4,'row_1'=8,'row_2'=2,'col'=4] {'row_0'}, dimensions={0}, use_global_device_ids=true | all-gather | bytes 327680 | tf_op jit(solution)/shard_map/all_gather | solution.py:31
  543.6 1.9 collective-permute-start.5
  547.5 9.0 %while.109 = (s32[]{:T(128)}, f32[384,256]{1,0:T(8,128)S(1)}, s32[]{:T(128)}, f32[4,128,64]{2,1,0:T(8,128)S(1)}, f32[4,64,64]{2,1,0:T(8,128)S(1)}, /*index=5*/s32[]{:T(128)}, s32[]{:T(128)}, s32[]{:T(128)}, s32[]{:T(128)}) while((s32[]{:T(128)}, f32[384,256]{1,0:T(8,128)S(1)}, s32[]{:T(128)}, f32[4,128,64]{2,1,0:T(8,128)S(1)}, ...), condition=%wide.region_11.12_spmd, body=%wide.region_10.11_spmd.sunk | while | flops 62947336 | bytes 1081519 | solution.py:61
  556.5 1.9 all-gather.30
  558.8 27.1 %all-gather.31 = f32[1024,128]{1,0:T(8,128)S(1)} all-gather(f32[128,128]{1,0:T(8,128)S(1)} %fusion.442), channel_id=33, replica_groups=mesh['row_0'=4,'row_1'=8,'row_2'=2,'col'=4] {'row_1'}, dimensions={0}, use_global_device_ids=true | all-gather | bytes 589824 | tf_op jit(solution)/shard_map/all_gather | solution.py:31
  586.0 1.9 all-gather.33
  588.4 25.3 %all-gather.34 = f32[1024,128]{1,0:T(8,128)S(1)} all-gather(f32[128,128]{1,0:T(8,128)S(1)} %convolution_add_fusion.49), channel_id=36, replica_groups=mesh['row_0'=4,'row_1'=8,'row_2'=2,'col'=4] {'row_1'}, dimensions={0}, use_global_device_ids=true | all-gather | bytes 589824 | tf_op jit(solution)/shard_map/all_gather | solution.py:31
  615.6 12.4 %all-gather.35 = f32[512,128]{1,0:T(8,128)S(1)} all-gather(f32[128,128]{1,0:T(8,128)S(1)} %convolution_add_fusion.42), channel_id=37, replica_groups=mesh['row_0'=4,'row_1'=8,'row_2'=2,'col'=4] {'row_0'}, dimensions={0}, use_global_device_ids=true | all-gather | bytes 327680 | tf_op jit(solution)/shard_map/all_gather | solution.py:31
  629.7 12.3 %all-gather.32 = f32[512,128]{1,0:T(8,128)S(1)} all-gather(f32[128,128]{1,0:T(8,128)S(1)} %fusion.437), channel_id=34, replica_groups=mesh['row_0'=4,'row_1'=8,'row_2'=2,'col'=4] {'row_0'}, dimensions={0}, use_global_device_ids=true | all-gather | bytes 327680 | tf_op jit(solution)/shard_map/all_gather | solution.py:31
  643.7 1.9 collective-permute-start.6
  647.6 9.4 %while.110 = (s32[]{:T(128)}, f32[384,256]{1,0:T(8,128)S(1)}, s32[]{:T(128)}, f32[4,128,64]{2,1,0:T(8,128)S(1)}, f32[4,64,64]{2,1,0:T(8,128)S(1)}, /*index=5*/s32[]{:T(128)}, s32[]{:T(128)}, s32[]{:T(128)}, s32[]{:T(128)}) while((s32[]{:T(128)}, f32[384,256]{1,0:T(8,128)S(1)}, s32[]{:T(128)}, f32[4,128,64]{2,1,0:T(8,128)S(1)}, ...), condition=%wide.region_13.14_spmd, body=%wide.region_12.13_spmd.sunk | while | flops 62947336 | bytes 1081519 | solution.py:61
  657.0 1.9 all-gather.36
  659.3 25.7 %all-gather.37 = f32[1024,128]{1,0:T(8,128)S(1)} all-gather(f32[128,128]{1,0:T(8,128)S(1)} %fusion.414), channel_id=39, replica_groups=mesh['row_0'=4,'row_1'=8,'row_2'=2,'col'=4] {'row_1'}, dimensions={0}, use_global_device_ids=true | all-gather | bytes 589824 | tf_op jit(solution)/shard_map/all_gather | solution.py:31
  685.1 1.9 all-gather.39
  687.5 25.7 %all-gather.40 = f32[1024,128]{1,0:T(8,128)S(1)} all-gather(f32[128,128]{1,0:T(8,128)S(1)} %convolution_add_fusion.34), channel_id=42, replica_groups=mesh['row_0'=4,'row_1'=8,'row_2'=2,'col'=4] {'row_1'}, dimensions={0}, use_global_device_ids=true | all-gather | bytes 589824 | tf_op jit(solution)/shard_map/all_gather | solution.py:31
  715.0 12.6 %all-gather.41 = f32[512,128]{1,0:T(8,128)S(1)} all-gather(f32[128,128]{1,0:T(8,128)S(1)} %convolution_add_fusion.27), channel_id=43, replica_groups=mesh['row_0'=4,'row_1'=8,'row_2'=2,'col'=4] {'row_0'}, dimensions={0}, use_global_device_ids=true | all-gather | bytes 327680 | tf_op jit(solution)/shard_map/all_gather | solution.py:31
  729.3 12.3 %all-gather.38 = f32[512,128]{1,0:T(8,128)S(1)} all-gather(f32[128,128]{1,0:T(8,128)S(1)} %fusion.409), channel_id=40, replica_groups=mesh['row_0'=4,'row_1'=8,'row_2'=2,'col'=4] {'row_0'}, dimensions={0}, use_global_device_ids=true | all-gather | bytes 327680 | tf_op jit(solution)/shard_map/all_gather | solution.py:31
  743.3 1.9 collective-permute-start.7
  747.2 8.7 %while.111 = (s32[]{:T(128)}, f32[384,256]{1,0:T(8,128)S(1)}, s32[]{:T(128)}, f32[4,128,64]{2,1,0:T(8,128)S(1)}, f32[4,64,64]{2,1,0:T(8,128)S(1)}, /*index=5*/s32[]{:T(128)}, s32[]{:T(128)}, s32[]{:T(128)}, s32[]{:T(128)}) while((s32[]{:T(128)}, f32[384,256]{1,0:T(8,128)S(1)}, s32[]{:T(128)}, f32[4,128,64]{2,1,0:T(8,128)S(1)}, ...), condition=%wide.region_15.16_spmd, body=%wide.region_14.15_spmd.sunk | while | flops 62947336 | bytes 1081519 | solution.py:61
  755.9 1.9 all-gather.42
  758.2 25.8 %all-gather.43 = f32[1024,128]{1,0:T(8,128)S(1)} all-gather(f32[128,128]{1,0:T(8,128)S(1)} %fusion.386), channel_id=45, replica_groups=mesh['row_0'=4,'row_1'=8,'row_2'=2,'col'=4] {'row_1'}, dimensions={0}, use_global_device_ids=true | all-gather | bytes 589824 | tf_op jit(solution)/shard_map/all_gather | solution.py:31
  784.2 1.9 all-gather.45
  786.5 25.5 %all-gather.46 = f32[1024,128]{1,0:T(8,128)S(1)} all-gather(f32[128,128]{1,0:T(8,128)S(1)} %convolution_add_fusion.19), channel_id=48, replica_groups=mesh['row_0'=4,'row_1'=8,'row_2'=2,'col'=4] {'row_1'}, dimensions={0}, use_global_device_ids=true | all-gather | bytes 589824 | tf_op jit(solution)/shard_map/all_gather | solution.py:31
  813.9 12.3 %all-gather.47 = f32[512,128]{1,0:T(8,128)S(1)} all-gather(f32[128,128]{1,0:T(8,128)S(1)} %convolution_add_fusion.12), channel_id=49, replica_groups=mesh['row_0'=4,'row_1'=8,'row_2'=2,'col'=4] {'row_0'}, dimensions={0}, use_global_device_ids=true | all-gather | bytes 327680 | tf_op jit(solution)/shard_map/all_gather | solution.py:31
  827.9 12.3 %all-gather.44 = f32[512,128]{1,0:T(8,128)S(1)} all-gather(f32[128,128]{1,0:T(8,128)S(1)} %fusion.381), channel_id=46, replica_groups=mesh['row_0'=4,'row_1'=8,'row_2'=2,'col'=4] {'row_0'}, dimensions={0}, use_global_device_ids=true | all-gather | bytes 327680 | tf_op jit(solution)/shard_map/all_gather | solution.py:31
  (425 shorter events, 120.5 us)
Async XLA Ops:
  6.5 0.9 copy-start.1
  6.5 39.9 %all-gather.50.cloned.1.call-start = ((), (), s32[]{:S(2)}) async-start(), calls=%async_computation | async-start | bytes 1310720 | tf_op jit(solution)/shard_map/all_gather | solution.py:82
  7.3 18.6 %copy-start = (f32[8,1,64,64]{3,2,1,0:T(8,128)S(1)}, f32[8,1,64,64]{3,2,1,0:T(8,128)}, u32[]{:S(2)}) copy-start(f32[8,1,64,64]{3,2,1,0:T(8,128)} %param.23) | copy-start | bytes 393220
  7.5 1.9 copy-start.3
  7.5 38.9 %collective-permute-start = (f32[128,128]{1,0:T(8,128)S(1)}, f32[128,128]{1,0:T(8,128)S(1)}, u32[]{:S(2)}, u32[]{:S(2)}) collective-permute-start(f32[128,128]{1,0:T(8,128)S(1)} %get-tuple-element.900), channel_id=1, source_target_pairs={{4,0},{8,4},{12,8},{16,12},{20,16},{24,20},{28,24},{32,28},{36,32}... | collective-permute-start | bytes 196616 | tf_op jit(solution)/shard_map/ppermute | solution.py:17
  22.7 2.5 copy-start.2
  144.3 3.8 collective-permute-start.1
  245.3 3.8 collective-permute-start.2
  344.6 3.8 collective-permute-start.3
  444.2 3.8 collective-permute-start.4
  543.6 3.8 collective-permute-start.5
  643.7 3.8 collective-permute-start.6
  743.3 3.8 collective-permute-start.7
Sparse Core Ops, SparseCore 0:
  9.1 32.9 all-gather.49
where the time goes:
time: 860 us; the launch traced here: 850 us
  blocking collectives  663 us (77%)
  matrix products  72.6 us (8%)
  local copies, waits for them, and re-layouts  32.6 us (4%)
  between operations  31.2 us (4%)
  loops' own time  21.6 us (3%)
  starting transfers between devices  15.4 us (2%)
  waiting for transfers between devices  13 us (2%)
    all_gather x48, blocking collectives, carried_in(): pieces = jax.tree.map(lambda part: lax.all_gather(part, axis), subtotal)  643 us
    dynamic_update_slice x32, local copies, waits for them, and re-layouts, advance(): lax.dynamic_update_slice_in_dim(current, reflect(segment, householder, tr...  28.6 us
    dot_general x136, matrix products, compose(): jnp.dot(later[0], earlier[1], precision=highest, preferred_element_type=j...  27.4 us
    another operation x8, loops' own time, sweep_apply(): return lax.fori_loop(0, house_set.shape[0], advance, extended)  21.6 us
    all_gather x1, blocking collectives, local(): lax.all_gather(factors, 'col', axis=1, tiled=True)  20.4 us
    dot_general x96, matrix products, compose(): jnp.dot(later[0], earlier[0], precision=highest, preferred_element_type=j...  19.2 us
  transfers between devices with their start and end apart: 9, of which 7 were waited for; matrix products, arithmetic and copies ran while one was open for 0% of the time, Pallas kernels for 0%

commit v1 on v0

v1 whole, which is shorter than its diff:
```python
import functools

import jax
import jax.numpy as jnp
from jax import lax
from jax.experimental import pallas as pl
from jax.experimental.pallas import tpu as pltpu
from jax.sharding import Mesh
from jax.sharding import PartitionSpec as P

ROW = ("x", "z", "core")
ROW_COL = ("x", "z", "core", "y")
MESH = pl.DeviceIdType.MESH
F32 = jnp.float32
BF16 = jnp.bfloat16
NB = 64
HI = lax.Precision.HIGHEST
VM = pltpu.VMEM


def dot_f32(a, b):
    return jnp.dot(a, b, precision=HI, preferred_element_type=F32)


def halves(a):
    high = a.astype(BF16)
    return high, (a - high.astype(F32)).astype(BF16)


def dot3(a_high, a_low, b_high, b_low):
    product = functools.partial(jnp.dot, preferred_element_type=F32)
    return product(a_high, b_high) + (product(a_high, b_low) + product(a_low, b_high))


def packed(a):
    n = a.shape[0] // 2
    return jnp.concatenate([a[:n], a[n:]], axis=1)


def unpacked(a):
    return jnp.concatenate([a[:, :NB], a[:, NB:]], axis=0)


def beside(a, b):
    return jnp.concatenate([a, b], axis=1)


def barrier(devices):
    semaphore = pltpu.get_barrier_semaphore()
    for device in devices:
        pl.semaphore_signal(semaphore, inc=1, device_id=device, device_id_type=MESH)
    pl.semaphore_wait(semaphore, len(devices))


def remote(source, target, sent, received, device):
    return pltpu.make_async_remote_copy(
        src_ref=source, dst_ref=target, send_sem=sent, recv_sem=received, device_id=device, device_id_type=MESH
    )


def gather_kernel(vt_ref, t_ref, gv_ref, gt_ref, tp_ref, sent, received):
    y = lax.axis_index("y")
    right, left, across = lax.rem(y + 1, 4), lax.rem(y + 3, 4), lax.rem(y + 2, 4)
    barrier([{"y": right}, {"y": left}])
    sends = []

    def start(source, target, k, side):
        copy = remote(source, target, sent.at[k], received.at[k], {"y": side})
        copy.start()
        sends.append(copy)

    start(vt_ref, gv_ref.at[y], 0, right)
    start(vt_ref, gv_ref.at[y], 1, left)
    half = t_ref.shape[0] // 2
    for k in range(half):
        tp_ref[k] = beside(t_ref[2 * k], t_ref[2 * k + 1])
    start(tp_ref, gt_ref.at[y], 2, right)
    start(tp_ref, gt_ref.at[y], 3, left)
    gv_ref[y] = vt_ref[...]
    gt_ref[y] = tp_ref[...]

    def arrived(target, k):
        remote(target, target, sent.at[k], received.at[k], {"y": right}).wait_recv()

    lower, upper = pl.ds(0, half), pl.ds(half, half)
    arrived(gv_ref.at[left], 0)
    start(gv_ref.at[left, lower], gv_ref.at[left, lower], 4, right)
    arrived(gv_ref.at[right], 1)
    start(gv_ref.at[right, upper], gv_ref.at[right, upper], 5, left)
    lower_t, upper_t = pl.ds(0, half // 2), pl.ds(half // 2, half // 2)
    arrived(gt_ref.at[left], 2)
    start(gt_ref.at[left, lower_t], gt_ref.at[left, lower_t], 6, right)
    arrived(gt_ref.at[right], 3)
    start(gt_ref.at[right, upper_t], gt_ref.at[right, upper_t], 7, left)
    arrived(gv_ref.at[across, lower], 4)
    arrived(gv_ref.at[across, upper], 5)
    arrived(gt_ref.at[across, lower_t], 6)
    arrived(gt_ref.at[across, upper_t], 7)
    for copy in sends:
        copy.wait_send()


def gather_blocks(vt, t):
    sweeps = vt.shape[0]
    return pl.pallas_call(
        gather_kernel,
        out_shape=[
            jax.ShapeDtypeStruct((4, sweeps, NB, 2 * NB), F32),
            jax.ShapeDtypeStruct((4, sweeps // 2, NB, 2 * NB), F32),
        ],
        in_specs=[pl.BlockSpec(memory_space=VM)] * 2,
        out_specs=[pl.BlockSpec(memory_space=VM)] * 2,
        scratch_shapes=[
            VM((sweeps // 2, NB, 2 * NB), F32),
            pltpu.SemaphoreType.DMA((8,)),
            pltpu.SemaphoreType.DMA((8,)),
        ],
        compiler_params=pltpu.CompilerParams(collective_id=0, has_side_effects=True),
        name="gather_blocks",
    )(vt, t)


def build_kernel(order_ref, gv_ref, gt_ref, out_ref):
    stored = order_ref[pl.program_id(0)]
    odd = lax.rem(stored, 2) == 1
    eye = (
        lax.broadcasted_iota(jnp.int32, (2 * NB, 2 * NB), 0) == lax.broadcasted_iota(jnp.int32, (2 * NB, 2 * NB), 1)
    ).astype(F32)
    carry = None
    for j in range(4):
        vt = gv_ref[j, 0]
        pair = gt_ref[j, 0]
        t = jnp.where(odd, pair[:, NB:], pair[:, :NB])
        w = dot_f32(t, vt)
        block = eye - lax.dot_general(vt, w, (((0,), (0,)), ((), ())), precision=HI, preferred_element_type=F32)
        if j == 0:
            rows = block
        else:
            rows = beside(dot_f32(block[:, :NB], carry), block[:, NB:])
        wide = rows.shape[1]
        out_ref[0, NB * j : NB * (j + 1), :] = jnp.concatenate(
            [rows[:NB], jnp.zeros((NB, 6 * NB - wide), F32)], axis=1
        )
        carry = rows[NB:]
    out_ref[0, 4 * NB :, :] = beside(carry, jnp.zeros((NB, NB), F32))


def build_maps(order, gv, gt):
    sweeps = gv.shape[1]
    return pl.pallas_call(
        build_kernel,
        out_shape=jax.ShapeDtypeStruct((sweeps, 5 * NB, 6 * NB), F32),
        grid_spec=pltpu.PrefetchScalarGridSpec(
            num_scalar_prefetch=1,
            grid=(sweeps,),
            in_specs=[
                pl.BlockSpec((4, 1, NB, 2 * NB), lambda p, order: (0, order[p], 0, 0)),
                pl.BlockSpec((4, 1, NB, 2 * NB), lambda p, order: (0, order[p] // 2, 0, 0)),
            ],
            out_specs=pl.BlockSpec((1, 5 * NB, 6 * NB), lambda p, order: (p, 0, 0)),
        ),
        name="build_maps",
    )(order, gv, gt)


class Place:
    def __init__(self):
        self.nx, self.nz = lax.axis_size("x"), lax.axis_size("z")
        self.x, self.z, self.core = lax.axis_index("x"), lax.axis_index("z"), lax.axis_index("core")
        chips = self.nx * self.nz
        self.chip = self.x * self.nz + self.z
        following, before = lax.rem(self.chip + 1, chips), lax.rem(self.chip + chips - 1, chips)
        self.following = {"x": following // self.nz, "z": lax.rem(following, self.nz)}
        self.before = {"x": before // self.nz, "z": lax.rem(before, self.nz)}
        self.partner = {"core": 1 - self.core}
        self.first = self.chip == 0
        self.last = self.chip == chips - 1

    def z_peers(self):
        return [{"z": lax.rem(self.z + d, self.nz)} for d in range(1, self.nz)]

    def x_peers(self):
        return [{"x": lax.rem(self.x + d, self.nx)} for d in range(1, self.nx)]

    def greet(self):
        barrier([self.partner, self.following, self.before] + self.z_peers() + self.x_peers())


def prepare_kernel(
    own_ref, mh_ref, ml_ref, reh_ref, rel_ref, rhh_ref, rhl_ref, pzh_ref, pzl_ref, pxh_ref, pxl_ref,
    other_ref, resp_ref, head_ref, next_ref, tz_ref, tx_ref, pz_ref, px_ref, sent, received, sent_z, received_z, sent_x, received_x,
):
    here = Place()
    nx, nz, core = here.nx, here.nz, here.core
    sweeps = own_ref.shape[0]
    mine = sweeps // 2
    here.greet()
    sends = []

    def start(source, target, send_sem, recv_sem, device):
        copy = remote(source, target, send_sem, recv_sem, device)
        copy.start()
        sends.append(copy)

    def arrived(target, send_sem, recv_sem):
        remote(target, target, send_sem, recv_sem, here.partner).wait_recv()

    start(own_ref, other_ref, sent.at[0], received.at[0], here.partner)

    def split_own(p, _):
        high, low = halves(own_ref[p])
        mh_ref[core, p] = high
        ml_ref[core, p] = low
        return 0

    lax.fori_loop(0, sweeps, split_own, 0)
    arrived(other_ref, sent.at[0], received.at[0])

    def respond(p, _):
        high, low = halves(other_ref[p])
        mh_ref[1 - core, p] = high
        ml_ref[1 - core, p] = low
        mine_first, other_first = own_ref[p, :, : 2 * NB], other_ref[p, :, : 2 * NB]
        first = jnp.where(core == 0, mine_first, other_first)[:, :NB]
        second = jnp.where(core == 0, other_first, mine_first)[:, :NB]
        resp_ref[p, : 4 * NB] = first[: 4 * NB]
        resp_ref[p, 4 * NB :] = dot_f32(second, first[4 * NB :])
        head_ref[p] = packed(first[: 2 * NB])
        return 0

    lax.fori_loop(0, sweeps, respond, 0)
    for k in range(mine // 2):
        p = mine * core + 2 * k
        tz_ref[here.z, k] = beside(resp_ref[p, 8 * NB :], resp_ref[p + 1, 8 * NB :])
    for d in range(1, nz):
        start(tz_ref.at[here.z], tz_ref.at[here.z], sent_z.at[d], received_z.at[here.z], {"z": lax.rem(here.z + d, nz)})
    start(head_ref, next_ref, sent.at[1], received.at[1], here.before)
    for d in range(1, nz):
        slot = lax.rem(here.z + d, nz)
        arrived(tz_ref.at[slot], sent_z.at[d], received_z.at[slot])

    eye = (lax.broadcasted_iota(jnp.int32, (NB, NB), 0) == lax.broadcasted_iota(jnp.int32, (NB, NB), 1)).astype(F32)

    def piece(ref, slot, k):
        pair = ref[slot, k // 2]
        return pair[:, NB:] if k % 2 else pair[:, :NB]

    whole, reach = [], []
    for k in range(mine):
        p = mine * core + k
        upto = jnp.zeros((NB, NB), F32)
        full = eye
        for slot in reversed(range(nz)):
            if slot < nz - 1:
                both = dot_f32(jnp.concatenate([upto, full], axis=0), piece(tz_ref, slot + 1, k))
                upto, full = both[:NB], both[NB:]
            upto = jnp.where(slot == here.z - 1, eye, upto)
            both = jnp.concatenate([upto, full], axis=0)
            at = slice(NB // 2 * slot, NB // 2 * (slot + 1))
            pz_ref[p, : 2 * NB, at] = both[:, : NB // 2]
            pz_ref[p, 2 * NB :, at] = both[:, NB // 2 :]
        both = dot_f32(jnp.concatenate([upto, full], axis=0), piece(tz_ref, 0, k))
        reach.append(jnp.where(here.z == 0, eye, both[:NB]))
        whole.append(both[NB:])
    for k in range(mine // 2):
        tx_ref[here.x, k] = beside(whole[2 * k], whole[2 * k + 1])
    for d in range(1, nx):
        start(tx_ref.at[here.x], tx_ref.at[here.x], sent_x.at[d], received_x.at[here.x], {"x": lax.rem(here.x + d, nx)})
    positions = pl.ds(mine * core, mine)
    start(pz_ref.at[positions], pz_ref.at[positions], sent.at[2], received.at[2], here.partner)

    arrived(next_ref, sent.at[1], received.at[1])

    def extend(p, _):
        ahead = unpacked(next_ref[p])
        rhh_ref[p], rhl_ref[p] = halves(ahead)
        resp = resp_ref[p]
        reh_ref[p, : 8 * NB], rel_ref[p, : 8 * NB] = halves(resp[: 8 * NB])
        reh_ref[p, 8 * NB :], rel_ref[p, 8 * NB :] = halves(dot_f32(ahead, resp[8 * NB :]))
        return 0

    lax.fori_loop(0, sweeps, extend, 0)

    for d in range(1, nx):
        slot = lax.rem(here.x + d, nx)
        arrived(tx_ref.at[slot], sent_x.at[d], received_x.at[slot])
    for k in range(mine):
        p = mine * core + k
        upto = jnp.zeros((NB, NB), F32)
        for slot in reversed(range(nx)):
            if slot < nx - 1:
                upto = dot_f32(upto, piece(tx_ref, slot + 1, k))
            upto = jnp.where(slot == here.x - 1, reach[k], upto)
            at = slice(NB // 2 * slot, NB // 2 * (slot + 1))
            px_ref[p, :NB, at] = upto[:, : NB // 2]
            px_ref[p, NB:, at] = upto[:, NB // 2 :]
    start(px_ref.at[positions], px_ref.at[positions], sent.at[3], received.at[3], here.partner)
    others = pl.ds(mine * (1 - core), mine)
    arrived(pz_ref.at[others], sent.at[2], received.at[2])
    arrived(px_ref.at[others], sent.at[3], received.at[3])

    def split_carry(p, _):
        pzh_ref[p], pzl_ref[p] = halves(pz_ref[p])
        pxh_ref[p], pxl_ref[p] = halves(px_ref[p])
        return 0

    lax.fori_loop(0, sweeps, split_carry, 0)
    for copy in sends:
        copy.wait_send()


def prepare(maps, nx, nz):
    sweeps = maps.shape[0]
    half = NB // 2

    def pair(*shape):
        return [jax.ShapeDtypeStruct(shape, BF16)] * 2

    outs = (
        pair(2, sweeps, 5 * NB, 6 * NB)
        + pair(sweeps, 10 * NB, NB)
        + pair(sweeps, 2 * NB, NB)
        + pair(sweeps, 4 * NB, half * nz)
        + pair(sweeps, 2 * NB, half * nx)
    )
    return pl.pallas_call(
        prepare_kernel,
        out_shape=outs,
        in_specs=[pl.BlockSpec(memory_space=VM)],
        out_specs=[pl.BlockSpec(memory_space=VM)] * len(outs),
        scratch_shapes=[
            VM(maps.shape, F32),
            VM((sweeps, 9 * NB, NB), F32),
            VM((sweeps, NB, 2 * NB), F32),
            VM((sweeps, NB, 2 * NB), F32),
            VM((nz, sweeps // 4, NB, 2 * NB), F32),
            VM((nx, sweeps // 4, NB, 2 * NB), F32),
            VM((sweeps, 4 * NB, half * nz), F32),
            VM((sweeps, 2 * NB, half * nx), F32),
            pltpu.SemaphoreType.DMA((4,)),
            pltpu.SemaphoreType.DMA((4,)),
            pltpu.SemaphoreType.DMA((nz,)),
            pltpu.SemaphoreType.DMA((nz,)),
            pltpu.SemaphoreType.DMA((nx,)),
            pltpu.SemaphoreType.DMA((nx,)),
        ],
        compiler_params=pltpu.CompilerParams(
            collective_id=1, has_side_effects=True, vmem_limit_bytes=60 * 1024 * 1024
        ),
        name="prepare",
    )(maps)


ABOVE = 2 * NB
OWN = 8 * NB


def sweep_kernel(
    shifts_ref, eig_ref, mh_ref, ml_ref, reh_ref, rel_ref, rhh_ref, rhl_ref, pzh_ref, pzl_ref, pxh_ref, pxl_ref, out_ref,
    rows_ref, turn_ref, turned_ref, edge_ref, edges_ref, sums_ref, totals_ref, ends_ref, heads_ref, y_ref,
    sent, received, sent_z, received_z, sent_x, received_x, sent_h, received_h,
):
    here = Place()
    nx, nz, core = here.nx, here.nz, here.core
    sweeps = mh_ref.shape[1]
    here.greet()

    def arrived(target, send_sem, recv_sem):
        remote(target, target, send_sem, recv_sem, here.partner).wait_recv()

    mine = eig_ref[...]
    turned = jnp.where(core == 0, mine, pltpu.roll(mine, NB, 1))
    turn_ref[...] = packed(turned[:, NB:])
    to_partner = remote(turn_ref, turned_ref.at[0], sent.at[0], received.at[0], here.partner)
    to_partner.start()
    rows_ref[...] = jnp.zeros_like(rows_ref)
    kept = turned[:, :NB]
    arrived(turned_ref.at[0], sent.at[0], received.at[0])
    got = unpacked(turned_ref[0])
    rows_ref[ABOVE : ABOVE + OWN] = jnp.concatenate(
        [jnp.where(core == 0, kept, got), jnp.where(core == 0, got, kept)], axis=0
    )
    edge_ref[sweeps] = packed(rows_ref[ABOVE : ABOVE + 2 * NB])
    to_before = remote(edge_ref.at[sweeps], edges_ref.at[sweeps], sent_h.at[sweeps], received_h.at[sweeps], here.before)
    to_before.start()
    arrived(edges_ref.at[sweeps], sent_h.at[sweeps], received_h.at[sweeps])
    rows_ref[ABOVE + OWN : ABOVE + OWN + 2 * NB] = unpacked(edges_ref[sweeps])
    to_partner.wait_send()
    to_before.wait_send()

    index = lax.broadcasted_iota(jnp.int32, (10 * NB, NB), 0)

    def sweep(p, _):
        shift = shifts_ref[p, 0]
        offset = shifts_ref[p, 1]
        window = rows_ref[pl.ds(NB + shift, 10 * NB), :]
        beyond = jnp.logical_and(here.last, index >= 9 * NB - offset)
        carried = jnp.logical_and(jnp.logical_not(here.first), jnp.logical_and(index >= NB, index < 2 * NB))
        inputs = jnp.where(jnp.logical_or(beyond, carried), 0.0, window)
        head = window[:NB]
        high, low = halves(inputs[NB : 7 * NB])
        end_a = dot3(mh_ref[0, p, 4 * NB :], ml_ref[0, p, 4 * NB :], high, low)
        second = jnp.concatenate([end_a, inputs[6 * NB :], jnp.zeros((NB, NB), F32)], axis=0)
        high_b, low_b = halves(second)
        end_b = dot3(mh_ref[1, p, 4 * NB :], ml_ref[1, p, 4 * NB :], high_b, low_b)
        sums_ref[p, here.z] = packed(end_b)
        z_copies = []
        for d in range(1, nz):
            copy = remote(
                sums_ref.at[p, here.z], sums_ref.at[p, here.z], sent_z.at[p, d], received_z.at[p, here.z],
                {"z": lax.rem(here.z + d, nz)},
            )
            copy.start()
            z_copies.append(copy)
        body_a = dot3(mh_ref[0, p, : 4 * NB], ml_ref[0, p, : 4 * NB], high, low)
        edge_ref[p] = packed(body_a[: 2 * NB])
        h_copy = remote(edge_ref.at[p], edges_ref.at[p], sent_h.at[p], received_h.at[p], here.before)
        h_copy.start()
        y_ref[: 4 * NB] = body_a
        y_ref[4 * NB : 8 * NB] = dot3(mh_ref[1, p, : 4 * NB], ml_ref[1, p, : 4 * NB], high_b, low_b)
        end_high, end_low = halves(end_b)
        ahead = dot3(rhh_ref[p], rhl_ref[p], end_high, end_low)
        for d in range(1, nz):
            slot = lax.rem(here.z + d, nz)
            arrived(sums_ref.at[p, slot], sent_z.at[p, d], received_z.at[p, slot])
        high_z, low_z = halves(sums_ref[p].reshape(nz * NB // 2, 2 * NB))
        both = dot3(pzh_ref[p], pzl_ref[p], high_z, low_z)
        combined = both[: 2 * NB, :NB] + both[2 * NB :, NB:]
        totals_ref[p, here.x] = packed(combined[NB:])
        x_copies = []
        for d in range(1, nx):
            copy = remote(
                totals_ref.at[p, here.x], totals_ref.at[p, here.x], sent_x.at[p, d], received_x.at[p, here.x],
                {"x": lax.rem(here.x + d, nx)},
            )
            copy.start()
            x_copies.append(copy)
        arrived(edges_ref.at[p], sent_h.at[p], received_h.at[p])
        y_ref[8 * NB :] = unpacked(edges_ref[p]) + ahead
        rows_ref[NB:ABOVE] = head
        for d in range(1, nx):
            slot = lax.rem(here.x + d, nx)
            arrived(totals_ref.at[p, slot], sent_x.at[p, d], received_x.at[p, slot])
        high_x, low_x = halves(totals_ref[p].reshape(nx * NB // 2, 2 * NB))
        both = dot3(pxh_ref[p], pxl_ref[p], high_x, low_x)
        carry = combined[:NB] + both[:NB, :NB] + both[NB:, NB:]
        carry_high, carry_low = halves(carry)
        rows_ref[ABOVE : ABOVE + 10 * NB] = y_ref[...] + dot3(reh_ref[p], rel_ref[p], carry_high, carry_low)
        for copy in z_copies + x_copies + [h_copy]:
            copy.wait_send()
        return 0

    lax.fori_loop(0, sweeps, sweep, 0)

    ends_ref[...] = packed(rows_ref[ABOVE + 7 * NB : ABOVE + 8 * NB])
    to_next = remote(ends_ref, heads_ref, sent.at[1], received.at[1], here.following)
    to_next.start()
    arrived(heads_ref, sent.at[1], received.at[1])
    rows_ref[NB:ABOVE] = jnp.where(here.first, rows_ref[NB:ABOVE], unpacked(heads_ref[...]))
    final = rows_ref[pl.ds(ABOVE - shifts_ref[sweeps - 1, 1], OWN), :]
    upper, lower = final[: 4 * NB], final[4 * NB :]
    turn_ref[...] = packed(jnp.where(core == 0, lower, upper))
    back = remote(turn_ref, turned_ref.at[1], sent.at[2], received.at[2], here.partner)
    back.start()
    kept = jnp.where(core == 0, upper, lower)
    arrived(turned_ref.at[1], sent.at[2], received.at[2])
    got = unpacked(turned_ref[1])
    out_ref[...] = beside(jnp.where(core == 0, kept, got), jnp.where(core == 0, got, kept))
    to_next.wait_send()
    back.wait_send()


def apply_sweeps(shifts, eigvecs, prepared, nx, nz):
    sweeps = shifts.shape[0]
    half = NB // 2
    dma = pltpu.SemaphoreType.DMA
    return pl.pallas_call(
        sweep_kernel,
        out_shape=jax.ShapeDtypeStruct(eigvecs.shape, F32),
        in_specs=[pl.BlockSpec(memory_space=pltpu.SMEM)] + [pl.BlockSpec(memory_space=VM)] * (1 + len(prepared)),
        out_specs=pl.BlockSpec(memory_space=VM),
        scratch_shapes=[
            VM((14 * NB, NB), F32),
            VM((2 * NB, 2 * NB), F32),
            VM((2, 2 * NB, 2 * NB), F32),
            VM((sweeps + 1, NB, 2 * NB), F32),
            VM((sweeps + 1, NB, 2 * NB), F32),
            VM((sweeps, nz, half, 2 * NB), F32),
            VM((sweeps, nx, half, 2 * NB), F32),
            VM((half, 2 * NB), F32),
            VM((half, 2 * NB), F32),
            VM((10 * NB, NB), F32),
            dma((3,)),
            dma((3,)),
            dma((sweeps, nz)),
            dma((sweeps, nz)),
            dma((sweeps, nx)),
            dma((sweeps, nx)),
            dma((sweeps + 1,)),
            dma((sweeps + 1,)),
        ],
        compiler_params=pltpu.CompilerParams(
            collective_id=2, has_side_effects=True, vmem_limit_bytes=60 * 1024 * 1024
        ),
        name="apply_sweeps",
    )(shifts, eigvecs, *prepared)


def solution(mesh):
    nz, cores, ny = 8, 2, mesh.shape["col"]
    nx = mesh.shape["row"] // (nz * cores)
    torus = Mesh(mesh.devices.reshape(nx, nz, cores, ny), ROW_COL)

    def local(eigvecs, reflectors, factors, order, offsets):
        transposed = jnp.swapaxes(reflectors[:, 0], 1, 2)
        gv, gt = gather_blocks(transposed, factors[:, 0])
        maps = build_maps(order, gv, gt)
        prepared = prepare(maps, nx, nz)
        used = offsets[order]
        previous = jnp.concatenate([jnp.zeros((1,), jnp.int32), used[:-1]])
        shifts = jnp.stack([used - previous, used], axis=1)
        return apply_sweeps(shifts, eigvecs, prepared, nx, nz)

    placed = (P(ROW, "y"), P(None, ROW_COL, None, None), P(None, ROW_COL, None, None), P(), P())
    return jax.shard_map(local, mesh=torus, in_specs=placed, out_specs=P(ROW, "y"), check_vma=False)
```

time: 860 us -> 201 us (0.23)
  the two profiles are of different devices: /device:TPU:32 before, /device:TPU:1 now
where the time goes in v1:
time: 201 us; the launch traced here: 200 us
  Pallas kernels  197 us (98%)
  local copies, waits for them, and re-layouts  2.91 us (1%)
    pallas_call x1, Pallas kernels, apply_sweeps(): pl.pallas_call(sweep_kernel, out_shape=jax.ShapeDtypeStruct(eigvecs.shape...  109 us
    pallas_call x1, Pallas kernels, prepare(): pl.pallas_call(prepare_kernel, out_shape=outs, in_specs=[pl.BlockSpec(mem...  53.3 us
    pallas_call x1, Pallas kernels, gather_blocks(): pl.pallas_call(gather_kernel, out_shape=[jax.ShapeDtypeStruct((4, sweeps,...  18.6 us
    pallas_call x1, Pallas kernels, build_maps(): pl.pallas_call(build_kernel, out_shape=jax.ShapeDtypeStruct((sweeps, 5 *...  16.7 us

profile of v1, /device:TPU:1, one launch (start us, length us, event | category | flops | bytes accessed | tf_op | source)
XLA Modules:
  0.0 200.3 jit_solution(15420605762402280713)
XLA Ops:
  0.0 0.0 copy-start
  0.0 18.6 %gather_blocks.1 = (f32[4,8,64,128]{3,2,1,0:T(8,128)}, f32[4,4,64,128]{3,2,1,0:T(8,128)}) custom-call(f32[8,64,128]{2,1,0:T(8,128)} %bitcast.8, f32[8,64,64]{2,1,0:T(8,128)} %bitcast.9), custom_call_target="tpu_custom_call" | custom-call | tf_op jit(solution)/shard_map/gather_blocks/pallas_call | solution.py:105
  18.6 0.0 copy-start.1
  18.6 16.7 %build_maps.1.own_ref = f32[8,320,384]{2,1,0:T(8,128)} custom-call(s32[8]{0:T(128)} %order_ref.1, f32[4,8,64,128]{3,2,1,0:T(8,128)} %get-tuple-element.17.gv_ref, f32[4,4,64,128]{3,2,1,0:T(8,128)} %get-tuple-element.18.gt_ref), custom_call_target="tpu_custom_call" | custom-call | tf_op jit(solution)/shard_map/build_maps/pallas_call | solution.py:150
  35.3 53.3 %prepare.1 = (bf16[2,8,320,384]{3,2,1,0:T(8,128)(2,1)}, bf16[2,8,320,384]{3,2,1,0:T(8,128)(2,1)}, bf16[8,640,64]{2,1,0:T(8,128)(2,1)}, bf16[8,640,64]{2,1,0:T(8,...) custom-call(f32[8,320,384]{2,1,0:T(8,128)} %build_maps.1.own_ref), custom_call_target="tpu_custom_call" | custom-call | tf_op jit(solution)/shard_map/prepare/pallas_call | solution.py:326
  88.6 0.0 copy-done.1
  88.7 0.0 copy-done
  88.7 0.6 gather_fusion
  89.3 0.1 add_subtract_fusion
  89.4 0.7 copy.12.shifts_ref
  90.1 108.6 %apply_sweeps.1 = f32[256,128]{1,0:T(8,128)} custom-call(s32[8,2]{1,0:T(8,128)} %copy.12.shifts_ref, f32[256,128]{1,0:T(8,128)} %eig_ref.1, bf16[2,8,320,384]{3,2,1,0:T(8,128)(2,1)} %get-tuple-element.19.mh_ref, bf16[2,8,320,384]{3,2,1,0:T(8,128)(2,1)} %get-tuple-element.20.ml_ref, bf16[8,640,64]{2,1,0:T(8,128)(2,1)} %get-tuple-element.21.reh_ref, ...), custom_call_target="tpu_custom_call" | custom-call | tf_op jit(solution)/shard_map/apply_sweeps/pallas_call | solution.py:477
  198.7 1.6 copy.14
  (4 shorter events, 0.0 us)
Async XLA Ops:
  0.0 88.7 %copy-start = (s32[8]{0:T(128)S(1)}, s32[8]{0:T(128)}, u32[]{:S(2)}) copy-start(s32[8]{0:T(128)} %param.9) | copy-start | bytes 100
  18.6 70.1 %copy-start.1 = (s32[8]{0:T(128)S(1)}, s32[8]{0:T(128)}, u32[]{:S(2)}) copy-start(s32[8]{0:T(128)} %order_ref.1) | copy-start | bytes 100

commit v2 on v0

v2 whole, which is shorter than its diff:
```python
import functools

import jax
import jax.numpy as jnp
from jax import lax
from jax.experimental import pallas as pl
from jax.experimental.pallas import tpu as pltpu
from jax.sharding import Mesh
from jax.sharding import PartitionSpec as P

ROW = ("x", "z", "core")
ROW_COL = ("x", "z", "core", "y")
MESH = pl.DeviceIdType.MESH
F32 = jnp.float32
BF16 = jnp.bfloat16
NB = 64
VM = pltpu.VMEM


def halves(a):
    high = a.astype(BF16)
    return high, (a - high.astype(F32)).astype(BF16)


def dot3(a_high, a_low, b_high, b_low):
    product = functools.partial(jnp.dot, preferred_element_type=F32)
    return product(a_high, b_high) + (product(a_high, b_low) + product(a_low, b_high))


def dot_split(a, b):
    return dot3(*halves(a), *halves(b))


def packed(a):
    n = a.shape[0] // 2
    return jnp.concatenate([a[:n], a[n:]], axis=1)


def unpacked(a):
    return jnp.concatenate([a[:, :NB], a[:, NB:]], axis=0)


def beside(a, b):
    return jnp.concatenate([a, b], axis=1)


def barrier(devices):
    semaphore = pltpu.get_barrier_semaphore()
    for device in devices:
        pl.semaphore_signal(semaphore, inc=1, device_id=device, device_id_type=MESH)
    pl.semaphore_wait(semaphore, len(devices))


def remote(source, target, sent, received, device):
    return pltpu.make_async_remote_copy(
        src_ref=source, dst_ref=target, send_sem=sent, recv_sem=received, device_id=device, device_id_type=MESH
    )


class Place:
    def __init__(self):
        self.nx, self.nz = lax.axis_size("x"), lax.axis_size("z")
        self.x, self.z, self.core = lax.axis_index("x"), lax.axis_index("z"), lax.axis_index("core")
        chips = self.nx * self.nz
        self.chip = self.x * self.nz + self.z
        following, before = lax.rem(self.chip + 1, chips), lax.rem(self.chip + chips - 1, chips)
        self.following = {"x": following // self.nz, "z": lax.rem(following, self.nz)}
        self.before = {"x": before // self.nz, "z": lax.rem(before, self.nz)}
        self.partner = {"core": 1 - self.core}
        self.first = self.chip == 0
        self.last = self.chip == chips - 1

    def z_peers(self):
        return [{"z": lax.rem(self.z + d, self.nz)} for d in range(1, self.nz)]

    def x_peers(self):
        return [{"x": lax.rem(self.x + d, self.nx)} for d in range(1, self.nx)]

    def y_peers(self):
        return [{"y": lax.rem(lax.axis_index("y") + d, 4)} for d in range(1, 4)]

    def greet(self):
        barrier([self.partner, self.following, self.before] + self.z_peers() + self.x_peers() + self.y_peers())


ABOVE = 2 * NB
OWN = 8 * NB
HALF = NB // 2


def sweeps_kernel(
    order_ref, offsets_ref, eig_ref, vt_ref, t_ref, out_ref,
    blocks_ref, own_ref, other_ref, mh_ref, ml_ref, resp_ref, reh_ref, rel_ref, head_ref, next_ref, rhh_ref, rhl_ref,
    tz_ref, tx_ref, reach_ref, pzh_ref, pzl_ref, pxh_ref, pxl_ref,
    rows_ref, turn_ref, turned_ref, edge_ref, edges_ref, sums_ref, totals_ref, ends_ref, y_ref,
    sent_y, received_y, sent_m, received_m, sent_n, received_n, sent_tz, received_tz, sent_tx, received_tx,
    sent, received, sent_z, received_z, sent_x, received_x, sent_h, received_h,
):
    here = Place()
    nx, nz, core, y = here.nx, here.nz, here.core, lax.axis_index("y")
    sweeps = vt_ref.shape[0]
    far = sorted(range(1, nz), key=lambda d: -min(d, nz - d))
    here.greet()

    def arrived(target, send_sem, recv_sem):
        remote(target, target, send_sem, recv_sem, here.partner).wait_recv()


    def block_copy(p, d):
        at = blocks_ref.at[y, p]
        return remote(at, at, sent_y.at[p, d], received_y.at[p, y], {"y": lax.rem(y + d, 4)})

    def map_copy(p):
        return remote(own_ref.at[p], other_ref.at[p], sent_m.at[p], received_m.at[p], here.partner)

    def head_copy(p):
        return remote(head_ref.at[p], next_ref.at[p], sent_n.at[p], received_n.at[p], here.before)

    def along_z(ref, p, d, send_sems, recv_sems):
        at = ref.at[p, here.z]
        return remote(at, at, send_sems.at[p, d], recv_sems.at[p, here.z], {"z": lax.rem(here.z + d, nz)})

    def along_x(ref, p, d, send_sems, recv_sems):
        at = ref.at[p, here.x]
        return remote(at, at, send_sems.at[p, d], recv_sems.at[p, here.x], {"x": lax.rem(here.x + d, nx)})

    def edge_copy(p):
        return remote(edge_ref.at[p], edges_ref.at[p], sent_h.at[p], received_h.at[p], here.before)

    def await_z(ref, p, send_sems, recv_sems):
        for d in range(1, nz):
            slot = lax.rem(here.z + d, nz)
            arrived(ref.at[p, slot], send_sems.at[p, d], recv_sems.at[p, slot])

    def await_x(ref, p, send_sems, recv_sems):
        for d in range(1, nx):
            slot = lax.rem(here.x + d, nx)
            arrived(ref.at[p, slot], send_sems.at[p, d], recv_sems.at[p, slot])


    eye = (lax.broadcasted_iota(jnp.int32, (NB, NB), 0) == lax.broadcasted_iota(jnp.int32, (NB, NB), 1)).astype(F32)
    wide_eye = (
        lax.broadcasted_iota(jnp.int32, (2 * NB, 2 * NB), 0) == lax.broadcasted_iota(jnp.int32, (2 * NB, 2 * NB), 1)
    ).astype(F32)

    def build(p):
        for d in range(1, 4):
            slot = lax.rem(y + d, 4)
            arrived(blocks_ref.at[slot, p], sent_y.at[p, d], received_y.at[p, slot])
        maps = []
        for j in range(4):
            vt = blocks_ref[j, p, :NB]
            t = unpacked(blocks_ref[j, p, NB:])
            vh, vl = halves(vt)
            wh, wl = halves(dot3(*halves(t), vh, vl))
            product = functools.partial(
                lax.dot_general, dimension_numbers=(((0,), (0,)), ((), ())), preferred_element_type=F32
            )
            maps.append(wide_eye - (product(vh, wh) + (product(vh, wl) + product(vl, wh))))
        carry = None
        for j in range(4):
            block = maps[j]
            rows = block if j == 0 else beside(dot_split(block[:, :NB], carry), block[:, NB:])
            done = jnp.concatenate([rows[:NB], jnp.zeros((NB, 6 * NB - rows.shape[1]), F32)], axis=1)
            own_ref[p, NB * j : NB * (j + 1), :] = done
            carry = rows[NB:]
        own_ref[p, 4 * NB :, :] = beside(carry, jnp.zeros((NB, NB), F32))
        map_copy(p).start()
        mh_ref[core, p], ml_ref[core, p] = halves(own_ref[p])

    def respond(p):
        arrived(other_ref.at[p], sent_m.at[p], received_m.at[p])
        mine_first, other_first = own_ref[p, :, : 2 * NB], other_ref[p, :, : 2 * NB]
        first = jnp.where(core == 0, mine_first, other_first)[:, :NB]
        second = jnp.where(core == 0, other_first, mine_first)[:, :NB]
        later = dot_split(second, first[4 * NB :])
        tz_ref[p, here.z] = packed(later[4 * NB :])
        for d in far:
            along_z(tz_ref, p, d, sent_tz, received_tz).start()
        head_ref[p] = packed(first[: 2 * NB])
        head_copy(p).start()
        resp_ref[p] = later[4 * NB :]
        reh_ref[p, : 4 * NB], rel_ref[p, : 4 * NB] = halves(first[: 4 * NB])
        reh_ref[p, 4 * NB : 8 * NB], rel_ref[p, 4 * NB : 8 * NB] = halves(later[: 4 * NB])
        mh_ref[1 - core, p], ml_ref[1 - core, p] = halves(other_ref[p])

    def chain_z(p):
        await_z(tz_ref, p, sent_tz, received_tz)
        both = jnp.concatenate([jnp.zeros((NB, NB), F32), eye], axis=0)
        upper = lax.broadcasted_iota(jnp.int32, (2 * NB, NB), 0) < NB
        twice = jnp.concatenate([eye, eye], axis=0)
        for slot in reversed(range(nz)):
            if slot < nz - 1:
                both = dot_split(both, unpacked(tz_ref[p, slot + 1]))
            both = jnp.where(jnp.logical_and(upper, slot == here.z - 1), twice, both)
            high, low = halves(both)
            at = slice(HALF * slot, HALF * (slot + 1))
            for ref, part in ((pzh_ref, high), (pzl_ref, low)):
                ref[p, : 2 * NB, at] = part[:, :HALF]
                ref[p, 2 * NB :, at] = part[:, HALF:]
        both = dot_split(both, unpacked(tz_ref[p, 0]))
        tx_ref[p, here.x] = packed(both[NB:])
        for d in range(1, nx):
            along_x(tx_ref, p, d, sent_tx, received_tx).start()
        reach_ref[p] = jnp.where(here.z == 0, eye, both[:NB])

    def chain_x(p):
        arrived(next_ref.at[p], sent_n.at[p], received_n.at[p])
        ahead = unpacked(next_ref[p])
        ahead_high, ahead_low = halves(ahead)
        rhh_ref[p], rhl_ref[p] = ahead_high, ahead_low
        reh_ref[p, 8 * NB :], rel_ref[p, 8 * NB :] = halves(dot3(ahead_high, ahead_low, *halves(resp_ref[p])))
        await_x(tx_ref, p, sent_tx, received_tx)
        upto = jnp.zeros((NB, NB), F32)
        for slot in reversed(range(nx)):
            if slot < nx - 1:
                upto = dot_split(upto, unpacked(tx_ref[p, slot + 1]))
            upto = jnp.where(slot == here.x - 1, reach_ref[p], upto)
            high, low = halves(upto)
            at = slice(HALF * slot, HALF * (slot + 1))
            for ref, part in ((pxh_ref, high), (pxl_ref, low)):
                ref[p, :NB, at] = part[:, :HALF]
                ref[p, NB:, at] = part[:, HALF:]


    mine = eig_ref[...]
    turned = jnp.where(core == 0, mine, pltpu.roll(mine, NB, 1))
    turn_ref[0] = packed(turned[:, NB:])
    to_partner = remote(turn_ref.at[0], turned_ref.at[0], sent.at[0], received.at[0], here.partner)
    to_partner.start()

    def give(p, _):
        stored = order_ref[p]
        blocks_ref[y, p, :NB] = vt_ref[stored]
        blocks_ref[y, p, NB:] = packed(t_ref[stored])
        for d in (2, 1, 3):
            block_copy(p, d).start()
        return 0

    lax.fori_loop(0, sweeps, give, 0)
    rows_ref[...] = jnp.zeros_like(rows_ref)
    kept = turned[:, :NB]
    arrived(turned_ref.at[0], sent.at[0], received.at[0])
    got = unpacked(turned_ref[0])
    rows_ref[ABOVE : ABOVE + OWN] = jnp.concatenate(
        [jnp.where(core == 0, kept, got), jnp.where(core == 0, got, kept)], axis=0
    )
    edge_ref[sweeps] = packed(rows_ref[ABOVE : ABOVE + 2 * NB])
    edge_copy(sweeps).start()
    build(0)
    build(1)
    respond(0)
    build(2)
    respond(1)
    arrived(edges_ref.at[sweeps], sent_h.at[sweeps], received_h.at[sweeps])
    rows_ref[ABOVE + OWN : ABOVE + OWN + 2 * NB] = unpacked(edges_ref[sweeps])
    chain_z(0)

    index = lax.broadcasted_iota(jnp.int32, (10 * NB, NB), 0)

    def sweep(p, before):
        offset = offsets_ref[order_ref[p]]
        shift = offset - before
        window = rows_ref[pl.ds(NB + shift, 10 * NB), :]
        beyond = jnp.logical_and(here.last, index >= 9 * NB - offset)
        carried = jnp.logical_and(jnp.logical_not(here.first), jnp.logical_and(index >= NB, index < 2 * NB))
        inputs = jnp.where(jnp.logical_or(beyond, carried), 0.0, window)
        head = window[:NB]
        high, low = halves(inputs[NB : 7 * NB])
        end_a = dot3(mh_ref[0, p, 4 * NB :], ml_ref[0, p, 4 * NB :], high, low)
        second = jnp.concatenate([end_a, inputs[6 * NB :], jnp.zeros((NB, NB), F32)], axis=0)
        high_b, low_b = halves(second)
        end_b = dot3(mh_ref[1, p, 4 * NB :], ml_ref[1, p, 4 * NB :], high_b, low_b)
        sums_ref[p, here.z] = packed(end_b)
        for d in far:
            along_z(sums_ref, p, d, sent_z, received_z).start()
        body_a = dot3(mh_ref[0, p, : 4 * NB], ml_ref[0, p, : 4 * NB], high, low)
        edge_ref[p] = packed(body_a[: 2 * NB])
        edge_copy(p).start()
        rows_ref[NB:ABOVE] = head
        y_ref[: 4 * NB] = body_a
        y_ref[4 * NB : 8 * NB] = dot3(mh_ref[1, p, : 4 * NB], ml_ref[1, p, : 4 * NB], high_b, low_b)
        chain_x(p)
        y_ref[8 * NB :] = dot3(rhh_ref[p], rhl_ref[p], *halves(unpacked(sums_ref[p, here.z])))

        if p + 1 < sweeps:
            chain_z(p + 1)

        if p + 2 < sweeps:
            respond(p + 2)

        await_z(sums_ref, p, sent_z, received_z)
        high_z, low_z = halves(sums_ref[p].reshape(nz * HALF, 2 * NB))
        both = dot3(pzh_ref[p], pzl_ref[p], high_z, low_z)
        combined = both[: 2 * NB, :NB] + both[2 * NB :, NB:]
        totals_ref[p, here.x] = packed(combined[NB:])
        for d in range(1, nx):
            along_x(totals_ref, p, d, sent_x, received_x).start()
        arrived(edges_ref.at[p], sent_h.at[p], received_h.at[p])
        y_ref[8 * NB :] = y_ref[8 * NB :] + unpacked(edges_ref[p])

        if p + 3 < sweeps:
            build(p + 3)

        await_x(totals_ref, p, sent_x, received_x)
        high_x, low_x = halves(totals_ref[p].reshape(nx * HALF, 2 * NB))
        both = dot3(pxh_ref[p], pxl_ref[p], high_x, low_x)
        carry = combined[:NB] + both[:NB, :NB] + both[NB:, NB:]
        carry_high, carry_low = halves(carry)
        rows_ref[ABOVE : ABOVE + 10 * NB] = y_ref[...] + dot3(reh_ref[p], rel_ref[p], carry_high, carry_low)
        return offset

    last_offset = jnp.int32(0)
    for p in range(sweeps):
        last_offset = sweep(p, last_offset)


    ends_ref[0] = packed(rows_ref[ABOVE + 7 * NB : ABOVE + 8 * NB])
    to_next = remote(ends_ref.at[0], ends_ref.at[1], sent.at[1], received.at[1], here.following)
    to_next.start()

    def finish(p, _):
        for d in range(1, 4):
            block_copy(p, d).wait_send()
        map_copy(p).wait_send()
        head_copy(p).wait_send()
        edge_copy(p).wait_send()
        for d in range(1, nz):
            along_z(tz_ref, p, d, sent_tz, received_tz).wait_send()
            along_z(sums_ref, p, d, sent_z, received_z).wait_send()
        for d in range(1, nx):
            along_x(tx_ref, p, d, sent_tx, received_tx).wait_send()
            along_x(totals_ref, p, d, sent_x, received_x).wait_send()
        return 0

    lax.fori_loop(0, sweeps, finish, 0)
    edge_copy(sweeps).wait_send()
    to_partner.wait_send()
    arrived(ends_ref.at[1], sent.at[1], received.at[1])
    rows_ref[NB:ABOVE] = jnp.where(here.first, rows_ref[NB:ABOVE], unpacked(ends_ref[1]))
    final = rows_ref[pl.ds(ABOVE - last_offset, OWN), :]
    upper, lower = final[: 4 * NB], final[4 * NB :]
    turn_ref[1] = packed(jnp.where(core == 0, lower, upper))
    back = remote(turn_ref.at[1], turned_ref.at[1], sent.at[2], received.at[2], here.partner)
    back.start()
    kept = jnp.where(core == 0, upper, lower)
    arrived(turned_ref.at[1], sent.at[2], received.at[2])
    got = unpacked(turned_ref[1])
    out_ref[...] = beside(jnp.where(core == 0, kept, got), jnp.where(core == 0, got, kept))
    to_next.wait_send()
    back.wait_send()


def apply_sweeps(order, offsets, eigvecs, transposed, factors, nx, nz):
    sweeps = order.shape[0]
    dma = pltpu.SemaphoreType.DMA
    maps = (sweeps, 5 * NB, 6 * NB)
    full = (sweeps, NB, 2 * NB)
    scratch = [
        VM((4, sweeps, NB + HALF, 2 * NB), F32),
        VM(maps, F32),
        VM(maps, F32),
        VM((2,) + maps, BF16),
        VM((2,) + maps, BF16),
        VM((sweeps, NB, NB), F32),
        VM((sweeps, 10 * NB, NB), BF16),
        VM((sweeps, 10 * NB, NB), BF16),
        VM(full, F32),
        VM(full, F32),
        VM((sweeps, 2 * NB, NB), BF16),
        VM((sweeps, 2 * NB, NB), BF16),
        VM((sweeps, nz, HALF, 2 * NB), F32),
        VM((sweeps, nx, HALF, 2 * NB), F32),
        VM((sweeps, NB, NB), F32),
        VM((sweeps, 4 * NB, HALF * nz), BF16),
        VM((sweeps, 4 * NB, HALF * nz), BF16),
        VM((sweeps, 2 * NB, HALF * nx), BF16),
        VM((sweeps, 2 * NB, HALF * nx), BF16),
        VM((14 * NB, NB), F32),
        VM((2, 2 * NB, 2 * NB), F32),
        VM((2, 2 * NB, 2 * NB), F32),
        VM((sweeps + 1, NB, 2 * NB), F32),
        VM((sweeps + 1, NB, 2 * NB), F32),
        VM((sweeps, nz, HALF, 2 * NB), F32),
        VM((sweeps, nx, HALF, 2 * NB), F32),
        VM((2, HALF, 2 * NB), F32),
        VM((10 * NB, NB), F32),
        dma((sweeps, 4)),
        dma((sweeps, 4)),
        dma((sweeps,)),
        dma((sweeps,)),
        dma((sweeps,)),
        dma((sweeps,)),
        dma((sweeps, nz)),
        dma((sweeps, nz)),
        dma((sweeps, nx)),
        dma((sweeps, nx)),
        dma((3,)),
        dma((3,)),
        dma((sweeps, nz)),
        dma((sweeps, nz)),
        dma((sweeps, nx)),
        dma((sweeps, nx)),
        dma((sweeps + 1,)),
        dma((sweeps + 1,)),
    ]
    scalar, vector = pl.BlockSpec(memory_space=pltpu.SMEM), pl.BlockSpec(memory_space=VM)
    return pl.pallas_call(
        sweeps_kernel,
        out_shape=jax.ShapeDtypeStruct(eigvecs.shape, F32),
        in_specs=[scalar] * 2 + [vector] * 3,
        out_specs=vector,
        scratch_shapes=scratch,
        compiler_params=pltpu.CompilerParams(
            collective_id=0, has_side_effects=True, vmem_limit_bytes=60 * 1024 * 1024
        ),
        name="apply_sweeps",
    )(order, offsets, eigvecs, transposed, factors)


def solution(mesh):
    nz, cores, ny = 8, 2, mesh.shape["col"]
    nx = mesh.shape["row"] // (nz * cores)
    torus = Mesh(mesh.devices.reshape(nx, nz, cores, ny), ROW_COL)

    def local(eigvecs, reflectors, factors, order, offsets):
        transposed = jnp.swapaxes(reflectors[:, 0], 1, 2)
        return apply_sweeps(order, offsets, eigvecs, transposed, factors[:, 0], nx, nz)

    placed = (P(ROW, "y"), P(None, ROW_COL, None, None), P(None, ROW_COL, None, None), P(), P())
    return jax.shard_map(local, mesh=torus, in_specs=placed, out_specs=P(ROW, "y"), check_vma=False)
```

time: 860 us -> 124 us (0.14)
  the two profiles are of different devices: /device:TPU:32 before, /device:TPU:1 now
where the time goes in v2:
time: 124 us
  Pallas kernels  123 us (99%)
  local copies, waits for them, and re-layouts  1.57 us (1%)
    pallas_call x1, Pallas kernels, apply_sweeps(): pl.pallas_call(sweeps_kernel, out_shape=jax.ShapeDtypeStruct(eigvecs.shap...  123 us

profile of v2, /device:TPU:1, one launch (start us, length us, event | category | flops | bytes accessed | tf_op | source)
XLA Modules:
  0.0 124.4 jit_solution(5956293479514604034)
XLA Ops:
  0.0 122.9 %apply_sweeps.1 = f32[256,128]{1,0:T(8,128)} custom-call(s32[8]{0:T(128)} %order_ref.1, s32[8]{0:T(128)} %offsets_ref.1, f32[256,128]{1,0:T(8,128)} %eig_ref.1, f32[8,64,128]{2,1,0:T(8,128)} %bitcast.4, f32[8,64,64]{2,1,0:T(8,128)} %bitcast.5), custom_call_target="tpu_custom_call" | custom-call | tf_op jit(solution)/shard_map/apply_sweeps/pallas_call | solution.py:408
  122.9 1.6 %copy.7 = f32[256,128]{1,0:T(8,128)} copy(f32[256,128]{1,0:T(8,128)} %apply_sweeps.1) | data formatting | bytes 262144

commit v3 on v2

--- a/solution.py
+++ b/solution.py
@@ -91,7 +91,7 @@
 def sweeps_kernel(
     order_ref, offsets_ref, eig_ref, vt_ref, t_ref, out_ref,
     blocks_ref, own_ref, other_ref, mh_ref, ml_ref, resp_ref, reh_ref, rel_ref, head_ref, next_ref, rhh_ref, rhl_ref,
-    tz_ref, tx_ref, reach_ref, pzh_ref, pzl_ref, pxh_ref, pxl_ref,
+    tz_ref, tx_ref, reach_ref, pzh_ref, pzl_ref, pxh_ref, pxl_ref, eh_ref, el_ref,
     rows_ref, turn_ref, turned_ref, edge_ref, edges_ref, sums_ref, totals_ref, ends_ref, y_ref,
     sent_y, received_y, sent_m, received_m, sent_n, received_n, sent_tz, received_tz, sent_tx, received_tx,
     sent, received, sent_z, received_z, sent_x, received_x, sent_h, received_h,
@@ -143,10 +143,19 @@
         lax.broadcasted_iota(jnp.int32, (2 * NB, 2 * NB), 0) == lax.broadcasted_iota(jnp.int32, (2 * NB, 2 * NB), 1)
     ).astype(F32)
 
+    def give(p):
+        stored = order_ref[p]
+        blocks_ref[y, p, :NB] = vt_ref[stored]
+        blocks_ref[y, p, NB:] = packed(t_ref[stored])
+        for d in (2, 1, 3):
+            block_copy(p, d).start()
+
     def build(p):
         for d in range(1, 4):
             slot = lax.rem(y + d, 4)
             arrived(blocks_ref.at[slot, p], sent_y.at[p, d], received_y.at[p, slot])
+        if p + 1 < sweeps:
+            give(p + 1)
         maps = []
         for j in range(4):
             vt = blocks_ref[j, p, :NB]
@@ -180,6 +189,11 @@
         head_ref[p] = packed(first[: 2 * NB])
         head_copy(p).start()
         resp_ref[p] = later[4 * NB :]
+        mine_last, other_last = own_ref[p, 4 * NB :, :], other_ref[p, 4 * NB :, :]
+        end_first = jnp.where(core == 0, mine_last, other_last)
+        end_second = jnp.where(core == 0, other_last, mine_last)
+        through = dot_split(end_second[:, :NB], end_first)
+        eh_ref[p], el_ref[p] = halves(jnp.concatenate([through[:, : 5 * NB], end_second[:, NB : 5 * NB]], axis=1))
         reh_ref[p, : 4 * NB], rel_ref[p, : 4 * NB] = halves(first[: 4 * NB])
         reh_ref[p, 4 * NB : 8 * NB], rel_ref[p, 4 * NB : 8 * NB] = halves(later[: 4 * NB])
         mh_ref[1 - core, p], ml_ref[1 - core, p] = halves(other_ref[p])
@@ -223,21 +237,13 @@
                 ref[p, NB:, at] = part[:, HALF:]
 
 
+    give(0)
     mine = eig_ref[...]
     turned = jnp.where(core == 0, mine, pltpu.roll(mine, NB, 1))
     turn_ref[0] = packed(turned[:, NB:])
     to_partner = remote(turn_ref.at[0], turned_ref.at[0], sent.at[0], received.at[0], here.partner)
     to_partner.start()
 
-    def give(p, _):
-        stored = order_ref[p]
-        blocks_ref[y, p, :NB] = vt_ref[stored]
-        blocks_ref[y, p, NB:] = packed(t_ref[stored])
-        for d in (2, 1, 3):
-            block_copy(p, d).start()
-        return 0
-
-    lax.fori_loop(0, sweeps, give, 0)
     rows_ref[...] = jnp.zeros_like(rows_ref)
     kept = turned[:, :NB]
     arrived(turned_ref.at[0], sent.at[0], received.at[0])
@@ -248,13 +254,9 @@
     edge_ref[sweeps] = packed(rows_ref[ABOVE : ABOVE + 2 * NB])
     edge_copy(sweeps).start()
     build(0)
-    build(1)
     respond(0)
-    build(2)
-    respond(1)
     arrived(edges_ref.at[sweeps], sent_h.at[sweeps], received_h.at[sweeps])
     rows_ref[ABOVE + OWN : ABOVE + OWN + 2 * NB] = unpacked(edges_ref[sweeps])
-    chain_z(0)
 
     index = lax.broadcasted_iota(jnp.int32, (10 * NB, NB), 0)
 
@@ -266,41 +268,38 @@
         carried = jnp.logical_and(jnp.logical_not(here.first), jnp.logical_and(index >= NB, index < 2 * NB))
         inputs = jnp.where(jnp.logical_or(beyond, carried), 0.0, window)
         head = window[:NB]
-        high, low = halves(inputs[NB : 7 * NB])
-        end_a = dot3(mh_ref[0, p, 4 * NB :], ml_ref[0, p, 4 * NB :], high, low)
-        second = jnp.concatenate([end_a, inputs[6 * NB :], jnp.zeros((NB, NB), F32)], axis=0)
-        high_b, low_b = halves(second)
-        end_b = dot3(mh_ref[1, p, 4 * NB :], ml_ref[1, p, 4 * NB :], high_b, low_b)
-        sums_ref[p, here.z] = packed(end_b)
+        high, low = halves(inputs[NB:])
+        sums_ref[p, here.z] = packed(dot3(eh_ref[p], el_ref[p], high, low))
         for d in far:
             along_z(sums_ref, p, d, sent_z, received_z).start()
-        body_a = dot3(mh_ref[0, p, : 4 * NB], ml_ref[0, p, : 4 * NB], high, low)
+        high_a, low_a = high[: 6 * NB], low[: 6 * NB]
+        body_a = dot3(mh_ref[0, p, : 4 * NB], ml_ref[0, p, : 4 * NB], high_a, low_a)
         edge_ref[p] = packed(body_a[: 2 * NB])
         edge_copy(p).start()
         rows_ref[NB:ABOVE] = head
         y_ref[: 4 * NB] = body_a
-        y_ref[4 * NB : 8 * NB] = dot3(mh_ref[1, p, : 4 * NB], ml_ref[1, p, : 4 * NB], high_b, low_b)
-        chain_x(p)
-        y_ref[8 * NB :] = dot3(rhh_ref[p], rhl_ref[p], *halves(unpacked(sums_ref[p, here.z])))
-
+        end_a = dot3(mh_ref[0, p, 4 * NB :], ml_ref[0, p, 4 * NB :], high_a, low_a)
+        second = jnp.concatenate([end_a, inputs[6 * NB :], jnp.zeros((NB, NB), F32)], axis=0)
+        y_ref[4 * NB : 8 * NB] = dot3(mh_ref[1, p, : 4 * NB], ml_ref[1, p, : 4 * NB], *halves(second))
+        if p == 0:
+            build(1)
+        chain_z(p)
         if p + 1 < sweeps:
-            chain_z(p + 1)
-
-        if p + 2 < sweeps:
-            respond(p + 2)
+            respond(p + 1)
 
         await_z(sums_ref, p, sent_z, received_z)
         high_z, low_z = halves(sums_ref[p].reshape(nz * HALF, 2 * NB))
         both = dot3(pzh_ref[p], pzl_ref[p], high_z, low_z)
         combined = both[: 2 * NB, :NB] + both[2 * NB :, NB:]
         totals_ref[p, here.x] = packed(combined[NB:])
-        for d in range(1, nx):
+        for d in sorted(range(1, nx), key=lambda d: -min(d, nx - d)):
             along_x(totals_ref, p, d, sent_x, received_x).start()
+        if p + 2 < sweeps:
+            build(p + 2)
+        chain_x(p)
+        ahead = dot3(rhh_ref[p], rhl_ref[p], *halves(unpacked(sums_ref[p, here.z])))
         arrived(edges_ref.at[p], sent_h.at[p], received_h.at[p])
-        y_ref[8 * NB :] = y_ref[8 * NB :] + unpacked(edges_ref[p])
-
-        if p + 3 < sweeps:
-            build(p + 3)
+        y_ref[8 * NB :] = unpacked(edges_ref[p]) + ahead
 
         await_x(totals_ref, p, sent_x, received_x)
         high_x, low_x = halves(totals_ref[p].reshape(nx * HALF, 2 * NB))
@@ -376,6 +375,8 @@
         VM((sweeps, 4 * NB, HALF * nz), BF16),
         VM((sweeps, 2 * NB, HALF * nx), BF16),
         VM((sweeps, 2 * NB, HALF * nx), BF16),
+        VM((sweeps, NB, 9 * NB), BF16),
+        VM((sweeps, NB, 9 * NB), BF16),
         VM((14 * NB, NB), F32),
         VM((2, 2 * NB, 2 * NB), F32),
         VM((2, 2 * NB, 2 * NB), F32),

time: 124 us -> 115 us (0.927)
  Pallas kernels: 123 us -> 113 us
    pallas_call x1, Pallas kernels: 123 us -> 113 us  [apply_sweeps(): pl.pallas_call(sweeps_kernel, out_shape=jax.ShapeDtypeStruct(eigvecs.shap...]
where the time goes in v3:
time: 115 us
  Pallas kernels  113 us (98%)
  local copies, waits for them, and re-layouts  1.57 us (1%)
    pallas_call x1, Pallas kernels, apply_sweeps(): pl.pallas_call(sweeps_kernel, out_shape=jax.ShapeDtypeStruct(eigvecs.shap...  113 us

profile of v3, /device:TPU:1, one launch (start us, length us, event | category | flops | bytes accessed | tf_op | source)
XLA Modules:
  0.0 115.0 jit_solution(17579575881747579213)
XLA Ops:
  0.0 113.5 %apply_sweeps.1 = f32[256,128]{1,0:T(8,128)} custom-call(s32[8]{0:T(128)} %order_ref.1, s32[8]{0:T(128)} %offsets_ref.1, f32[256,128]{1,0:T(8,128)} %eig_ref.1, f32[8,64,128]{2,1,0:T(8,128)} %bitcast.4, f32[8,64,64]{2,1,0:T(8,128)} %bitcast.5), custom_call_target="tpu_custom_call" | custom-call | tf_op jit(solution)/shard_map/apply_sweeps/pallas_call | solution.py:409
  113.5 1.6 %copy.7 = f32[256,128]{1,0:T(8,128)} copy(f32[256,128]{1,0:T(8,128)} %apply_sweeps.1) | data formatting | bytes 262144

commit v4 on v3

--- a/solution.py
+++ b/solution.py
@@ -29,6 +29,16 @@
 
 def dot_split(a, b):
     return dot3(*halves(a), *halves(b))
+
+
+def three_terms(a):
+    high, low = halves(a)
+    return jnp.concatenate([high, high, low], axis=1)
+
+
+def three_below(a):
+    high, low = halves(a)
+    return jnp.concatenate([high, low, high], axis=0)
 
 
 def packed(a):
@@ -90,7 +100,7 @@
 
 def sweeps_kernel(
     order_ref, offsets_ref, eig_ref, vt_ref, t_ref, out_ref,
-    blocks_ref, own_ref, other_ref, mh_ref, ml_ref, resp_ref, reh_ref, rel_ref, head_ref, next_ref, rhh_ref, rhl_ref,
+    blocks_ref, own_ref, other_ref, mh_ref, ml_ref, resp_ref, re_ref, head_ref, next_ref,
     tz_ref, tx_ref, reach_ref, pzh_ref, pzl_ref, pxh_ref, pxl_ref, eh_ref, el_ref,
     rows_ref, turn_ref, turned_ref, edge_ref, edges_ref, sums_ref, totals_ref, ends_ref, y_ref,
     sent_y, received_y, sent_m, received_m, sent_n, received_n, sent_tz, received_tz, sent_tx, received_tx,
@@ -161,11 +171,12 @@
             vt = blocks_ref[j, p, :NB]
             t = unpacked(blocks_ref[j, p, NB:])
             vh, vl = halves(vt)
-            wh, wl = halves(dot3(*halves(t), vh, vl))
-            product = functools.partial(
-                lax.dot_general, dimension_numbers=(((0,), (0,)), ((), ())), preferred_element_type=F32
+            w = dot3(*halves(t), vh, vl)
+            left = jnp.concatenate([vh, vh, vl], axis=0)
+            product = lax.dot_general(
+                left, three_below(w), (((0,), (0,)), ((), ())), preferred_element_type=F32
             )
-            maps.append(wide_eye - (product(vh, wh) + (product(vh, wl) + product(vl, wh))))
+            maps.append(wide_eye - product)
         carry = None
         for j in range(4):
             block = maps[j]
@@ -175,7 +186,6 @@
             carry = rows[NB:]
         own_ref[p, 4 * NB :, :] = beside(carry, jnp.zeros((NB, NB), F32))
         map_copy(p).start()
-        mh_ref[core, p], ml_ref[core, p] = halves(own_ref[p])
 
     def respond(p):
         arrived(other_ref.at[p], sent_m.at[p], received_m.at[p])
@@ -194,9 +204,10 @@
         end_second = jnp.where(core == 0, other_last, mine_last)
         through = dot_split(end_second[:, :NB], end_first)
         eh_ref[p], el_ref[p] = halves(jnp.concatenate([through[:, : 5 * NB], end_second[:, NB : 5 * NB]], axis=1))
-        reh_ref[p, : 4 * NB], rel_ref[p, : 4 * NB] = halves(first[: 4 * NB])
-        reh_ref[p, 4 * NB : 8 * NB], rel_ref[p, 4 * NB : 8 * NB] = halves(later[: 4 * NB])
+        re_ref[p, : 4 * NB] = three_terms(first[: 4 * NB])
+        re_ref[p, 4 * NB : 8 * NB] = three_terms(later[: 4 * NB])
         mh_ref[1 - core, p], ml_ref[1 - core, p] = halves(other_ref[p])
+        mh_ref[core, p], ml_ref[core, p] = halves(own_ref[p])
 
     def chain_z(p):
         await_z(tz_ref, p, sent_tz, received_tz)
@@ -210,20 +221,24 @@
             high, low = halves(both)
             at = slice(HALF * slot, HALF * (slot + 1))
             for ref, part in ((pzh_ref, high), (pzl_ref, low)):
-                ref[p, : 2 * NB, at] = part[:, :HALF]
-                ref[p, 2 * NB :, at] = part[:, HALF:]
+                ref[p, :NB, at] = part[NB:, :HALF]
+                ref[p, NB : 2 * NB, at] = part[NB:, HALF:]
+                ref[p, 2 * NB : 3 * NB, at] = part[:NB, :HALF]
+                ref[p, 3 * NB :, at] = part[:NB, HALF:]
         both = dot_split(both, unpacked(tz_ref[p, 0]))
         tx_ref[p, here.x] = packed(both[NB:])
         for d in range(1, nx):
             along_x(tx_ref, p, d, sent_tx, received_tx).start()
         reach_ref[p] = jnp.where(here.z == 0, eye, both[:NB])
 
-    def chain_x(p):
+    def ahead_of(p):
         arrived(next_ref.at[p], sent_n.at[p], received_n.at[p])
         ahead = unpacked(next_ref[p])
         ahead_high, ahead_low = halves(ahead)
-        rhh_ref[p], rhl_ref[p] = ahead_high, ahead_low
-        reh_ref[p, 8 * NB :], rel_ref[p, 8 * NB :] = halves(dot3(ahead_high, ahead_low, *halves(resp_ref[p])))
+        re_ref[p, 8 * NB :] = three_terms(dot3(ahead_high, ahead_low, *halves(resp_ref[p])))
+        y_ref[8 * NB :] = dot3(ahead_high, ahead_low, *halves(unpacked(sums_ref[p, here.z])))
+
+    def chain_x(p):
         await_x(tx_ref, p, sent_tx, received_tx)
         upto = jnp.zeros((NB, NB), F32)
         for slot in reversed(range(nx)):
@@ -286,27 +301,29 @@
         chain_z(p)
         if p + 1 < sweeps:
             respond(p + 1)
+        ahead_of(p)
 
         await_z(sums_ref, p, sent_z, received_z)
         high_z, low_z = halves(sums_ref[p].reshape(nz * HALF, 2 * NB))
-        both = dot3(pzh_ref[p], pzl_ref[p], high_z, low_z)
-        combined = both[: 2 * NB, :NB] + both[2 * NB :, NB:]
-        totals_ref[p, here.x] = packed(combined[NB:])
+        both = dot3(pzh_ref[p, : 2 * NB], pzl_ref[p, : 2 * NB], high_z, low_z)
+        totals_ref[p, here.x] = packed(both[:NB, :NB] + both[NB:, NB:])
         for d in sorted(range(1, nx), key=lambda d: -min(d, nx - d)):
             along_x(totals_ref, p, d, sent_x, received_x).start()
+        both = dot3(pzh_ref[p, 2 * NB :], pzl_ref[p, 2 * NB :], high_z, low_z)
+        near = both[:NB, :NB] + both[NB:, NB:]
         if p + 2 < sweeps:
             build(p + 2)
         chain_x(p)
-        ahead = dot3(rhh_ref[p], rhl_ref[p], *halves(unpacked(sums_ref[p, here.z])))
         arrived(edges_ref.at[p], sent_h.at[p], received_h.at[p])
-        y_ref[8 * NB :] = unpacked(edges_ref[p]) + ahead
+        y_ref[8 * NB :] = unpacked(edges_ref[p]) + y_ref[8 * NB :]
 
         await_x(totals_ref, p, sent_x, received_x)
         high_x, low_x = halves(totals_ref[p].reshape(nx * HALF, 2 * NB))
         both = dot3(pxh_ref[p], pxl_ref[p], high_x, low_x)
-        carry = combined[:NB] + both[:NB, :NB] + both[NB:, NB:]
-        carry_high, carry_low = halves(carry)
-        rows_ref[ABOVE : ABOVE + 10 * NB] = y_ref[...] + dot3(reh_ref[p], rel_ref[p], carry_high, carry_low)
+        carry = near + both[:NB, :NB] + both[NB:, NB:]
+        rows_ref[ABOVE : ABOVE + 10 * NB] = y_ref[...] + jnp.dot(
+            re_ref[p], three_below(carry), preferred_element_type=F32
+        )
         return offset
 
     last_offset = jnp.int32(0)
@@ -362,12 +379,9 @@
         VM((2,) + maps, BF16),
         VM((2,) + maps, BF16),
         VM((sweeps, NB, NB), F32),
-        VM((sweeps, 10 * NB, NB), BF16),
-        VM((sweeps, 10 * NB, NB), BF16),
+        VM((sweeps, 10 * NB, 3 * NB), BF16),
         VM(full, F32),
         VM(full, F32),
-        VM((sweeps, 2 * NB, NB), BF16),
-        VM((sweeps, 2 * NB, NB), BF16),
         VM((sweeps, nz, HALF, 2 * NB), F32),
         VM((sweeps, nx, HALF, 2 * NB), F32),
         VM((sweeps, NB, NB), F32),

time: 115 us -> 114 us (level)
    pallas_call x1, Pallas kernels: 113 us -> 112 us  [apply_sweeps(): pl.pallas_call(sweeps_kernel, out_shape=jax.ShapeDtypeStruct(eigvecs.shap...]
where the time goes in v4:
time: 114 us; the launch traced here: 113 us
  Pallas kernels  112 us (98%)
  local copies, waits for them, and re-layouts  1.57 us (1%)
    pallas_call x1, Pallas kernels, apply_sweeps(): pl.pallas_call(sweeps_kernel, out_shape=jax.ShapeDtypeStruct(eigvecs.shap...  112 us

profile of v4, /device:TPU:1, one launch (start us, length us, event | category | flops | bytes accessed | tf_op | source)
XLA Modules:
  0.0 113.5 jit_solution(8188474677162000269)
XLA Ops:
  0.0 111.9 %apply_sweeps.1 = f32[256,128]{1,0:T(8,128)} custom-call(s32[8]{0:T(128)} %order_ref.1, s32[8]{0:T(128)} %offsets_ref.1, f32[256,128]{1,0:T(8,128)} %eig_ref.1, f32[8,64,128]{2,1,0:T(8,128)} %bitcast.4, f32[8,64,64]{2,1,0:T(8,128)} %bitcast.5), custom_call_target="tpu_custom_call" | custom-call | tf_op jit(solution)/shard_map/apply_sweeps/pallas_call | solution.py:423
  111.9 1.6 %copy.7 = f32[256,128]{1,0:T(8,128)} copy(f32[256,128]{1,0:T(8,128)} %apply_sweeps.1) | data formatting | bytes 262144

commit v5 on v4

--- a/solution.py
+++ b/solution.py
@@ -54,10 +54,11 @@
     return jnp.concatenate([a, b], axis=1)
 
 
-def barrier(devices):
+def barrier(devices, meanwhile):
     semaphore = pltpu.get_barrier_semaphore()
     for device in devices:
         pl.semaphore_signal(semaphore, inc=1, device_id=device, device_id_type=MESH)
+    meanwhile()
     pl.semaphore_wait(semaphore, len(devices))
 
 
@@ -89,8 +90,8 @@
     def y_peers(self):
         return [{"y": lax.rem(lax.axis_index("y") + d, 4)} for d in range(1, 4)]
 
-    def greet(self):
-        barrier([self.partner, self.following, self.before] + self.z_peers() + self.x_peers() + self.y_peers())
+    def greet(self, meanwhile):
+        barrier([self.partner, self.following, self.before] + self.z_peers() + self.x_peers() + self.y_peers(), meanwhile)
 
 
 ABOVE = 2 * NB
@@ -110,7 +111,22 @@
     nx, nz, core, y = here.nx, here.nz, here.core, lax.axis_index("y")
     sweeps = vt_ref.shape[0]
     far = sorted(range(1, nz), key=lambda d: -min(d, nz - d))
-    here.greet()
+
+    def own_block(p):
+        stored = order_ref[p]
+        blocks_ref[y, p, :NB] = vt_ref[stored]
+        blocks_ref[y, p, NB:] = packed(t_ref[stored])
+
+    def local_start():
+        mine = eig_ref[...]
+        turned = jnp.where(core == 0, mine, pltpu.roll(mine, NB, 1))
+        turn_ref[0] = packed(turned[:, NB:])
+        y_ref[: 4 * NB] = turned[:, :NB]
+        for p in range(sweeps):
+            own_block(p)
+        rows_ref[...] = jnp.zeros_like(rows_ref)
+
+    here.greet(local_start)
 
     def arrived(target, send_sem, recv_sem):
         remote(target, target, send_sem, recv_sem, here.partner).wait_recv()
@@ -154,9 +170,6 @@
     ).astype(F32)
 
     def give(p):
-        stored = order_ref[p]
-        blocks_ref[y, p, :NB] = vt_ref[stored]
-        blocks_ref[y, p, NB:] = packed(t_ref[stored])
         for d in (2, 1, 3):
             block_copy(p, d).start()
 
@@ -253,14 +266,10 @@
 
 
     give(0)
-    mine = eig_ref[...]
-    turned = jnp.where(core == 0, mine, pltpu.roll(mine, NB, 1))
-    turn_ref[0] = packed(turned[:, NB:])
     to_partner = remote(turn_ref.at[0], turned_ref.at[0], sent.at[0], received.at[0], here.partner)
     to_partner.start()
 
-    rows_ref[...] = jnp.zeros_like(rows_ref)
-    kept = turned[:, :NB]
+    kept = y_ref[: 4 * NB]
     arrived(turned_ref.at[0], sent.at[0], received.at[0])
     got = unpacked(turned_ref[0])
     rows_ref[ABOVE : ABOVE + OWN] = jnp.concatenate(

time: 114 us -> 114 us (level)
  no operation moved by 1% of the time
where the time goes in v5:
time: 114 us
  Pallas kernels  112 us (98%)
  local copies, waits for them, and re-layouts  1.57 us (1%)
    pallas_call x1, Pallas kernels, apply_sweeps(): pl.pallas_call(sweeps_kernel, out_shape=jax.ShapeDtypeStruct(eigvecs.shap...  112 us

profile of v5, /device:TPU:1, one launch (start us, length us, event | category | flops | bytes accessed | tf_op | source)
XLA Modules:
  0.0 114.0 jit_solution(13863626164283258937)
XLA Ops:
  0.0 112.4 %apply_sweeps.1 = f32[256,128]{1,0:T(8,128)} custom-call(s32[8]{0:T(128)} %order_ref.1, s32[8]{0:T(128)} %offsets_ref.1, f32[256,128]{1,0:T(8,128)} %eig_ref.1, f32[8,64,128]{2,1,0:T(8,128)} %bitcast.4, f32[8,64,64]{2,1,0:T(8,128)} %bitcast.5), custom_call_target="tpu_custom_call" | custom-call | tf_op jit(solution)/shard_map/apply_sweeps/pallas_call | solution.py:432
  112.4 1.6 %copy.7 = f32[256,128]{1,0:T(8,128)} copy(f32[256,128]{1,0:T(8,128)} %apply_sweeps.1) | data formatting | bytes 262144
